TPU v7x, 256 devices: a whole 4x4x8 slice. The times are simulated.
256 devices in a mesh: seq: 64 (over x, z, core), head: 4 (over y).
Axes of the slice: x: 4, y: 4, z: 8, core: 2. Of those that a mesh axis runs over, the one named last changes fastest.
Arguments:
- queries: bfloat16 [16384, 2048], P('seq', 'head'), may hold values from -1.75 to 1.75
- keys: bfloat16 [16384, 2048], P('seq', 'head'), may hold values from -1.75 to 1.75
- values: bfloat16 [16384, 2048], P('seq', 'head'), may hold values from -6 to 6
- level_table: float32 [16, 16], P(None, 'head'), may hold values from 0.05 to 1
- level_code: int32 [16384, 9], P('seq'), may hold values from 0 to 15
- out_weight: bfloat16 [2048, 2048], P('head'), may hold values from -0.125 to 0.125
- cotangent: bfloat16 [16384, 2048], P('seq', 'head'), may hold values from -16 to 16
Outputs:
- mixed: bfloat16 [16384, 2048], P('seq', 'head')
- out_weight_grad: float32 [2048, 2048], P('seq', 'head')
- query_grad: bfloat16 [16384, 2048], P('seq', 'head')
- key_grad: bfloat16 [16384, 2048], P('seq', 'head')
- value_grad: bfloat16 [16384, 2048], P('seq', 'head')
- table_grad: float32 [16, 16], P(None, 'head')
All inputs are finite; a program needn't handle non-finite values.
Results may differ from a plain program's by a relative error of at most 0.015.
Values may be sent and summed in bfloat16 or wider, within the bound.
A program may use at most 128 MiB of HBM per device.

v0:
```python
import math

import jax
import jax.numpy as jnp
from jax import lax
from jax.sharding import PartitionSpec as P

SPAN = 64


HIGHEST_PRECISION = lax.Precision.HIGHEST


def partner_2(value, axis, apart):
    mask = 2**apart
    pairs = [(source, source ^ mask) for source in range(lax.axis_size(axis))]
    return lax.ppermute(value, axis, pairs)


def laid_out(tiles, dim):
    tiles = jnp.moveaxis(tiles, 0, dim)
    lengths = tiles.shape
    return tiles.reshape(*lengths[:dim], lengths[dim] * lengths[dim + 1], *lengths[dim + 2 :])


def copy_for_each(shard, axis):
    devices = lax.axis_size(axis)
    return lax.all_to_all(
        jnp.broadcast_to(shard[None], (devices, *shard.shape)), axis, 0, 0, tiled=True
    )


def collect(shard, axis, dim):
    return laid_out(copy_for_each(shard, axis), dim)


def cut_along(shard, dim, devices):
    before, after = (shard.shape[:dim], shard.shape[dim + 1 :])
    return jnp.moveaxis(shard.reshape(*before, devices, -1, *after), dim, 0)


def sent_and_summed(shard, axis, dim):
    tiles = cut_along(shard, dim, lax.axis_size(axis))
    arrived = lax.all_to_all(tiles, axis, split_axis=0, concat_axis=0, tiled=True)
    return arrived.astype(jnp.float32).sum(axis=0)


def taken_together(shard, axis):
    everything = copy_for_each(shard, axis)
    return jnp.sum(everything, axis=0)


def split_einsum(form, left, right):
    if left.dtype == jnp.float32:
        high = left.astype(jnp.bfloat16)
        rest = (left - high.astype(jnp.float32)).astype(jnp.bfloat16)
        return jnp.einsum(form, high, right, preferred_element_type=jnp.float32) + jnp.einsum(
            form, rest, right, preferred_element_type=jnp.float32
        )
    high = right.astype(jnp.bfloat16)
    rest = (right - high.astype(jnp.float32)).astype(jnp.bfloat16)
    return jnp.einsum(form, left, high, preferred_element_type=jnp.float32) + jnp.einsum(
        form, left, rest, preferred_element_type=jnp.float32
    )


def upper_half(array, bit_index):
    group_size = 2 ** (bit_index + 1)
    grouped = array.reshape((array.shape[0] // group_size, group_size) + array.shape[1:])
    return grouped[:, group_size // 2 :]


def lower_sum(array, bit_index):
    group_size = 2 ** (bit_index + 1)
    grouped = array.reshape((array.shape[0] // group_size, group_size) + array.shape[1:])
    return jnp.sum(grouped[:, : group_size // 2], axis=1)


def place_upper(piece_array, bit_index):
    group_size = 2 ** (bit_index + 1)
    joined = jnp.concatenate([jnp.zeros_like(piece_array), piece_array], axis=1)
    return joined.reshape((piece_array.shape[0] * group_size,) + piece_array.shape[2:])


def spread_lower(piece_array, bit_index):
    group_size = 2 ** (bit_index + 1)
    filled = jnp.broadcast_to(
        piece_array[:, None], (piece_array.shape[0], group_size // 2) + piece_array.shape[1:]
    )
    joined = jnp.concatenate([filled, jnp.zeros_like(filled)], axis=1)
    return joined.reshape((piece_array.shape[0] * group_size,) + piece_array.shape[1:])


def both_blocks(device_state, device_terms, position, seq_bits):
    carried = jnp.concatenate([device_state[None], device_terms], axis=0)
    found_states = []
    gathered = jnp.zeros_like(device_state)
    for bit_index in range(seq_bits):
        partner = partner_2(carried.astype(jnp.bfloat16), "seq", bit_index).astype(carried.dtype)
        bit_owned = (position >> bit_index & 1).astype(jnp.float32)
        found_states.append(partner[0] * bit_owned)
        gathered = gathered + (1.0 - bit_owned) * partner[1]
        carried = jnp.concatenate([carried[:1] + partner[:1], carried[2:] + partner[2:]], axis=0)
    return (found_states, gathered)


def per_device(queries, keys, values, level_table, level_code, out_weight, cotangent):
    tok_rows = queries.shape[0]
    heads_here = level_table.shape[1]
    head_size = queries.shape[1] // heads_here
    span_len = SPAN
    spans_here = tok_rows // span_len
    local_bits = spans_here.bit_length() - 1
    seq_count = lax.axis_size("seq")
    seq_bits = seq_count.bit_length() - 1
    level_count = 1 + local_bits + seq_bits
    position = lax.axis_index("seq")
    four_shape = (spans_here, span_len, heads_here, head_size)
    scales = [
        1.0 / math.sqrt(span_len * 2 ** max(level_index - 1, 0))
        for level_index in range(level_count)
    ]
    code_count = level_table.shape[0]
    one_hot = (
        level_code[:, :, None] == jnp.arange(code_count, dtype=jnp.int32)[None, None, :]
    ).astype(jnp.float32)
    lookup = jnp.einsum("tlc,ch->tlh", one_hot, level_table, precision=HIGHEST_PRECISION)
    lookup = lookup.reshape(spans_here, span_len, level_count, heads_here)
    level_coef = lookup * jnp.asarray(scales, jnp.float32)[None, None, :, None]
    full_rows = collect(cotangent, "head", 1)
    grad_attn = jnp.einsum(
        "tj,ij->ti", full_rows, out_weight, preferred_element_type=jnp.float32
    ).astype(jnp.bfloat16)
    q_half = queries.reshape(four_shape)
    k_half = keys.reshape(four_shape)
    v_half = values.reshape(four_shape)
    g_half = grad_attn.reshape(four_shape)
    causal = (jnp.arange(span_len)[:, None] >= jnp.arange(span_len)[None, :]).astype(jnp.float32)
    scores = (
        jnp.einsum("jchd,jshd->jhcs", q_half, k_half, preferred_element_type=jnp.float32) * causal
    )
    level_reads = [split_einsum("jhcs,jshe->jche", scores, v_half) * scales[0]]
    span_states = jnp.einsum("jchd,jche->jhde", k_half, v_half, preferred_element_type=jnp.float32)
    local_lower = []
    for bit_index in range(local_bits):
        lower_state = lower_sum(span_states, bit_index)
        local_lower.append(lower_state)
        upper_reads = split_einsum("gjchd,ghde->gjche", upper_half(q_half, bit_index), lower_state)
        level_reads.append(place_upper(upper_reads, bit_index) * scales[1 + bit_index])
    device_state = jnp.sum(span_states, axis=0)
    scaled_seq = g_half[:, :, None] * level_coef[:, :, 1 + local_bits :, :, None]
    device_terms = split_einsum("jchd,jclhe->lhde", q_half, scaled_seq)
    found_states, gathered = both_blocks(device_state, device_terms, position, seq_bits)
    for bit_index in range(seq_bits):
        level_reads.append(
            split_einsum("jchd,hde->jche", q_half, found_states[bit_index])
            * scales[1 + local_bits + bit_index]
        )
    attention = jnp.zeros(four_shape, jnp.float32)
    for level_index in range(level_count):
        attention = attention + lookup[:, :, level_index, :, None] * level_reads[level_index]
    attn_rows = attention.reshape(tok_rows, heads_here * head_size).astype(jnp.bfloat16)
    partial_value = jnp.dot(attn_rows, out_weight, preferred_element_type=jnp.float32)
    mixed = sent_and_summed(partial_value.astype(jnp.bfloat16), "head", 1).astype(jnp.bfloat16)
    weight_norm = 1.0 / math.sqrt(tok_rows * seq_count)
    out_weight_grad = sent_and_summed(
        (
            jnp.einsum("tj,ti->ji", full_rows, attn_rows, preferred_element_type=jnp.float32)
            * weight_norm
        ).astype(jnp.bfloat16),
        "seq",
        0,
    )
    level_grads = jnp.stack(
        [jnp.sum(g_half * level_reads[level_index], axis=3) for level_index in range(level_count)],
        axis=2,
    )
    table_norm = 1.0 / math.sqrt(tok_rows * seq_count * level_count)
    table_part = (
        jnp.einsum(
            "tlc,tlh->ch",
            one_hot,
            level_grads.reshape(tok_rows, level_count, heads_here),
            precision=HIGHEST_PRECISION,
        )
        * table_norm
    )
    table_grad = taken_together(table_part, "seq")
    within_coef = jnp.transpose(level_coef[:, :, 0, :], (0, 2, 1))[:, :, :, None]
    score_grads = (
        jnp.einsum("jche,jshe->jhcs", g_half, v_half, preferred_element_type=jnp.float32)
        * causal
        * within_coef
    )
    query_grad = split_einsum("jhcs,jshd->jchd", score_grads, k_half)
    key_grad = split_einsum("jhcs,jchd->jshd", score_grads, q_half)
    value_grad = split_einsum("jhcs,jche->jshe", scores * within_coef, g_half)
    upper_terms = jnp.zeros_like(span_states)
    for bit_index in range(local_bits):
        coef_here = level_coef[:, :, 1 + bit_index, :, None]
        query_part = upper_half(coef_here, bit_index) * split_einsum(
            "gjche,ghde->gjchd", upper_half(g_half, bit_index), local_lower[bit_index]
        )
        query_grad = query_grad + place_upper(query_part, bit_index)
        scaled_grads = upper_half(g_half * coef_here, bit_index)
        block_terms = split_einsum("gjchd,gjche->ghde", upper_half(q_half, bit_index), scaled_grads)
        upper_terms = upper_terms + spread_lower(block_terms, bit_index)
    for bit_index in range(seq_bits):
        coef_here = level_coef[:, :, 1 + local_bits + bit_index, :, None]
        query_grad = query_grad + coef_here * split_einsum(
            "jche,hde->jchd", g_half, found_states[bit_index]
        )
    states_back = upper_terms + gathered[None]
    key_grad = key_grad + split_einsum("jhde,jche->jchd", states_back, v_half)
    value_grad = value_grad + split_einsum("jhde,jchd->jche", states_back, k_half)
    flat_shape = (tok_rows, heads_here * head_size)
    return (
        mixed,
        out_weight_grad,
        query_grad.reshape(flat_shape).astype(jnp.bfloat16),
        key_grad.reshape(flat_shape).astype(jnp.bfloat16),
        value_grad.reshape(flat_shape).astype(jnp.bfloat16),
        table_grad,
    )


def solution(mesh):
    placed = (
        P("seq", "head"),
        P("seq", "head"),
        P("seq", "head"),
        P(None, "head"),
        P("seq", None),
        P("head", None),
        P("seq", "head"),
    )
    return jax.shard_map(
        per_device,
        mesh=mesh,
        in_specs=placed,
        out_specs=(
            P("seq", "head"),
            P("seq", "head"),
            P("seq", "head"),
            P("seq", "head"),
            P("seq", "head"),
            P(None, "head"),
        ),
        check_vma=False,
    )
```

profile of v0, /device:TPU:1, one launch (start us, length us, event | category | flops | bytes accessed | tf_op | source)
XLA Modules:
  0.0 281.2 jit_solution(722215330220643382)
XLA Ops:
  0.7 1.2 copy.287
  1.9 1.0 broadcast_in_dim.11
  2.9 5.1 %all-to-all-start = ((bf16[4,256,512]{1,2,0:T(8,128)(2,1)}), bf16[4,256,512]{1,2,0:T(8,128)(2,1)}, u32[]{:S(2)}, u32[]{:S(2)}) async-start(bf16[4,256,512]{1,2,0:T(8,128)(2,1)} %broadcast_in_dim.11), calls=%async_computation | async-start | bytes 2097152 | tf_op jit(solution)/shard_map/all_to_all | solution.py:28
  10.5 2.1 fusion.173
  12.7 1.0 fusion.152
  15.5 1.8 copy.286
  17.3 1.6 bitcast_convert_fusion.5
  24.2 1.7 reshape.252
  27.4 1.1 copy.295
  29.7 1.8 concatenate.43.clone
  31.5 1.8 fusion.76
  34.4 1.1 fusion.110
  35.5 2.7 convolution_convert_fusion.1
  38.2 1.1 broadcast_in_dim_reshape.3
  39.2 1.8 reshape_reshape.16
  41.1 1.7 reshape_reshape.17
  45.7 2.6 fusion.2
  48.3 3.2 %fusion.172 = (bf16[6,4,128,128]{2,3,0,1:T(8,128)(2,1)S(1)}, f32[6,4,128,128]{2,3,0,1:T(8,128)}) fusion(bf16[4,64,4,128,1]{3,2,1,0,4:T(4,128)(2,1)S(1)} %bitcast.580, f32[4,64,6,4]{1,0,2,3:T(4,128)S(1)} %copy-done.75, f32[4,6,128,128,1]{3,2,4,1,0:T(8,128)S(1)} %fusion.2, bf16[4,64,4,128]{3,2,1,0:T(4,128)(2,1)S(1)} %broadcast_in_dim_reshape.3), kind=kOutput, calls=%fused_computation.320 | convolution fusion | flops 206176256 | bytes 4481024 | tf_op jit(solution)/shard_map/jchd,jclhe->lhde/dot_general | solution.py:62
  52.5 2.5 collective-permute-start
  56.6 1.3 fusion.12
  57.9 2.0 copy.460
  60.0 2.1 concatenate.53.clone
  62.4 1.0 fusion.37
  63.5 1.8 copy.395
  65.3 1.4 fusion.25
  66.6 1.4 fusion.35
  69.8 1.1 fusion.87
  71.8 1.2 fusion.60
  73.1 1.5 convert_element_type.323
  76.8 1.0 fusion.187
  77.8 15.9 %collective-permute-done.1 = bf16[6,4,128,128]{2,3,0,1:T(8,128)(2,1)S(1)} collective-permute-done((bf16[6,4,128,128]{2,3,0,1:T(8,128)(2,1)S(1)}, bf16[6,4,128,128]{2,3,0,1:T(8,128)(2,1)S(1)}, u32[]{:S(2)}, u32[]{:S(2)}) %collective-permute-start.1) | collective-permute-done | bytes 786464 | tf_op jit(solution)/shard_map/ppermute | solution.py:17
  94.3 2.1 collective-permute-start.2
  96.6 1.0 fusion.188
  98.9 26.8 %collective-permute-done.2 = bf16[5,4,128,128]{2,3,0,1:T(8,128)(2,1)S(1)} collective-permute-done((bf16[5,4,128,128]{2,3,0,1:T(8,128)(2,1)S(1)}, bf16[5,4,128,128]{2,3,0,1:T(8,128)(2,1)S(1)}, u32[]{:S(2)}, u32[]{:S(2)}) %collective-permute-start.2) | collective-permute-done | bytes 655392 | tf_op jit(solution)/shard_map/ppermute | solution.py:17
  126.1 5.5 %collective-permute-start.3 = (bf16[4,4,128,128]{2,3,0,1:T(8,128)(2,1)S(1)}, bf16[4,4,128,128]{2,3,0,1:T(8,128)(2,1)S(1)}, u32[]{:S(2)}, u32[]{:S(2)}) collective-permute-start(bf16[4,4,128,128]{2,3,0,1:T(8,128)(2,1)S(1)} %pad_maximum_fusion.3), channel_id=1, source_target_pairs={{0,32},{4,36},{8,40},{12,44},{16,48},{20,52},{24,56},{28,60},{32,0... | collective-permute-start | bytes 1572872 | tf_op jit(solution)/shard_map/ppermute | solution.py:17
  132.1 21.9 %collective-permute-done.3 = bf16[4,4,128,128]{2,3,0,1:T(8,128)(2,1)S(1)} collective-permute-done((bf16[4,4,128,128]{2,3,0,1:T(8,128)(2,1)S(1)}, bf16[4,4,128,128]{2,3,0,1:T(8,128)(2,1)S(1)}, u32[]{:S(2)}, u32[]{:S(2)}) %collective-permute-start.3) | collective-permute-done | bytes 524320 | tf_op jit(solution)/shard_map/ppermute | solution.py:17
  154.4 1.5 collective-permute-start.4
  156.5 6.9 %collective-permute-done.4 = bf16[3,4,128,128]{2,3,0,1:T(8,128)(2,1)S(1)} collective-permute-done((bf16[3,4,128,128]{2,3,0,1:T(8,128)(2,1)S(1)}, bf16[3,4,128,128]{2,3,0,1:T(8,128)(2,1)S(1)}, u32[]{:S(2)}, u32[]{:S(2)}) %collective-permute-start.4) | collective-permute-done | bytes 393248 | tf_op jit(solution)/shard_map/ppermute | solution.py:17
  163.6 3.3 %collective-permute-start.5 = (bf16[2,4,128,128]{2,3,0,1:T(8,128)(2,1)S(1)}, bf16[2,4,128,128]{2,3,0,1:T(8,128)(2,1)S(1)}, u32[]{:S(2)}, u32[]{:S(2)}) collective-permute-start(bf16[2,4,128,128]{2,3,0,1:T(8,128)(2,1)S(1)} %pad_maximum_fusion.5), channel_id=1, source_target_pairs={{0,128},{4,132},{8,136},{12,140},{16,144},{20,148},{24,152},{28,15... | collective-permute-start | bytes 786440 | tf_op jit(solution)/shard_map/ppermute | solution.py:17
  167.6 3.1 %collective-permute-done.5 = bf16[2,4,128,128]{2,3,0,1:T(8,128)(2,1)S(1)} collective-permute-done((bf16[2,4,128,128]{2,3,0,1:T(8,128)(2,1)S(1)}, bf16[2,4,128,128]{2,3,0,1:T(8,128)(2,1)S(1)}, u32[]{:S(2)}, u32[]{:S(2)}) %collective-permute-start.5) | collective-permute-done | bytes 262176 | tf_op jit(solution)/shard_map/ppermute | solution.py:17
  172.6 2.6 fusion.51
  175.2 1.4 fusion.49
  178.4 13.0 %all-to-all-start.3 = ((f32[64,16,4]{1,2,0:T(4,128)}), f32[64,16,4]{1,2,0:T(4,128)}, u32[]{:S(2)}, u32[]{:S(2)}) async-start(f32[64,16,4]{1,2,0:T(4,128)} %broadcast_in_dim.14), calls=%async_computation.3 | async-start | bytes 262144 | tf_op jit(solution)/shard_map/all_to_all | solution.py:28
  191.4 1.2 copy.336
  193.3 1.1 copy.691
  194.3 7.3 %all-to-all-done.3 = f32[64,16,4]{1,2,0:T(4,128)} async-done(((f32[64,16,4]{1,2,0:T(4,128)}), f32[64,16,4]{1,2,0:T(4,128)}, u32[]{:S(2)}, u32[]{:S(2)}) %all-to-all-start.3) | async-done | bytes 16416 | tf_op jit(solution)/shard_map/all_to_all | solution.py:28
  201.6 4.5 %all-to-all-start.1 = ((bf16[4,256,512]{2,1,0:T(8,128)(2,1)}), bf16[4,256,512]{2,1,0:T(8,128)(2,1)}, u32[]{:S(2)}, u32[]{:S(2)}) async-start(bf16[4,256,512]{2,1,0:T(8,128)(2,1)} %bitcast.606), calls=%async_computation.1 | async-start | bytes 2097152 | tf_op jit(solution)/shard_map/all_to_all | solution.py:44
  206.2 1.9 fusion.190
  208.1 1.9 fusion.191
  210.0 3.4 %fusion.1 = bf16[2048,512]{0,1:T(8,128)(2,1)} fusion(bf16[256,2048]{0,1:T(8,128)(2,1)} %bitcast.24, bf16[32,8,4,128]{3,2,1,0:T(4,128)(2,1)S(1)} %bitcast.609), kind=kOutput, calls=%fused_computation.5 | convolution fusion | flops 538968064 | bytes 3407872 | tf_op jit(solution)/shard_map/tj,ti->ji/dot_general | solution.py:168
  213.4 3.9 %copy.338 = bf16[2048,512]{1,0:T(8,128)(2,1)} copy(bf16[2048,512]{0,1:T(8,128)(2,1)} %fusion.1) | data formatting | bytes 4194304 | tf_op jit(solution)/shard_map/convert_element_type | solution.py:170
  217.3 3.5 %all-to-all-done.1 = bf16[4,256,512]{2,1,0:T(8,128)(2,1)} async-done(((bf16[4,256,512]{2,1,0:T(8,128)(2,1)}), bf16[4,256,512]{2,1,0:T(8,128)(2,1)}, u32[]{:S(2)}, u32[]{:S(2)}) %all-to-all-start.1) | async-done | bytes 1048608 | tf_op jit(solution)/shard_map/all_to_all | solution.py:44
  220.8 6.6 %all-to-all-start.2 = ((bf16[64,32,512]{2,1,0:T(8,128)(2,1)}), bf16[64,32,512]{2,1,0:T(8,128)(2,1)}, u32[]{:S(2)}, u32[]{:S(2)}) async-start(bf16[64,32,512]{2,1,0:T(8,128)(2,1)} %bitcast.578), calls=%async_computation.2 | async-start | bytes 4194304 | tf_op jit(solution)/shard_map/all_to_all | solution.py:44
  227.4 1.0 fusion.192
  228.5 1.0 fusion.193
  229.5 1.0 fusion.194
  231.6 1.4 fusion.64
  233.8 1.0 broadcast_in_dim.13
  234.8 1.6 subtract_convert_fusion
  241.4 1.2 fusion.30
  244.4 1.6 reduce_sum.149
  245.9 2.2 reduce_sum.138
  248.1 30.5 %all-to-all-done.2 = bf16[64,32,512]{2,1,0:T(8,128)(2,1)} async-done(((bf16[64,32,512]{2,1,0:T(8,128)(2,1)}), bf16[64,32,512]{2,1,0:T(8,128)(2,1)}, u32[]{:S(2)}, u32[]{:S(2)}) %all-to-all-start.2) | async-done | bytes 2097184 | tf_op jit(solution)/shard_map/all_to_all | solution.py:44
  278.6 2.5 convert_reduce_fusion
  (316 shorter events, 41.0 us)
Async XLA Ops:
  0.6 34.8 %copy-start = (bf16[512,2048]{1,0:T(8,128)(2,1)S(1)}, bf16[512,2048]{1,0:T(8,128)(2,1)}, u32[]{:S(2)}) copy-start(bf16[512,2048]{1,0:T(8,128)(2,1)} %param.13) | copy-start | bytes 6291460
  0.6 7.4 %copy-start.26 = (bf16[256,512]{1,0:T(8,128)(2,1)S(1)}, bf16[256,512]{1,0:T(8,128)(2,1)}, u32[]{:S(2)}) copy-start(bf16[256,512]{1,0:T(8,128)(2,1)} %param.8) | copy-start | bytes 786436
  2.9 6.7 %copy-start.71 = (bf16[256,512]{1,0:T(8,128)(2,1)S(1)}, bf16[256,512]{1,0:T(8,128)(2,1)}, u32[]{:S(2)}) copy-start(bf16[256,512]{1,0:T(8,128)(2,1)} %param.9) | copy-start | bytes 786436
  2.9 6.7 %copy-start.72 = (bf16[256,512]{1,0:T(8,128)(2,1)S(1)}, bf16[256,512]{1,0:T(8,128)(2,1)}, u32[]{:S(2)}) copy-start(bf16[256,512]{1,0:T(8,128)(2,1)} %param.10) | copy-start | bytes 786436
  2.9 32.5 %all-to-all-start = ((bf16[4,256,512]{1,2,0:T(8,128)(2,1)}), bf16[4,256,512]{1,2,0:T(8,128)(2,1)}, u32[]{:S(2)}, u32[]{:S(2)}) async-start(bf16[4,256,512]{1,2,0:T(8,128)(2,1)} %broadcast_in_dim.11), calls=%async_computation | async-start | bytes 2097152 | tf_op jit(solution)/shard_map/all_to_all | solution.py:28
  10.5 4.1 %copy-start.73 = (s32[256,9]{0,1:T(8,128)S(1)}, s32[256,9]{0,1:T(8,128)}, u32[]{:S(2)}) copy-start(s32[256,9]{0,1:T(8,128)} %param.12) | copy-start | bytes 27652
  10.5 4.1 %copy-start.94 = (f32[16,4]{0,1:T(4,128)S(1)}, f32[16,4]{0,1:T(4,128)}, u32[]{:S(2)}) copy-start(f32[16,4]{0,1:T(4,128)} %param.11) | copy-start | bytes 772
  12.5 14.8 %copy-start.4 = (f32[4,4,128,128]{3,2,1,0:T(8,128)}, f32[4,4,128,128]{3,2,1,0:T(8,128)S(1)}, u32[]{:S(2)}) copy-start(f32[4,4,128,128]{3,2,1,0:T(8,128)S(1)} %get-tuple-element.65) | copy-start | bytes 3145732
  14.6 6.4 %copy-start.95 = (f32[9]{0:T(128)S(1)}, f32[9]{0:T(128)}, u32[]{:S(2)}) copy-start(f32[9]{0:T(128)} %constant.50.clone) | copy-start | bytes 112
  17.3 3.7 %copy-start.70 = (f32[4,64,9,4]{1,0,3,2:T(4,128)S(1)}, f32[4,64,9,4]{1,0,3,2:T(4,128)}, u32[]{:S(2)}) copy-start(f32[4,64,9,4]{1,0,3,2:T(4,128)} %reshape.255) | copy-start | bytes 110596
  27.4 5.9 %copy-start.18 = (bf16[4,64,4,128]{3,2,1,0:T(4,128)(2,1)S(1)}, bf16[4,64,4,128]{3,2,1,0:T(4,128)(2,1)}, u32[]{:S(2)}) copy-start(bf16[4,64,4,128]{3,2,1,0:T(4,128)(2,1)} %reshape.252) | copy-start | bytes 786436
  27.4 5.9 %copy-start.69 = (f32[64,64]{1,0:T(8,128)S(1)}, f32[64,64]{1,0:T(8,128)}, u32[]{:S(2)}) copy-start(f32[64,64]{1,0:T(8,128)} %fusion.137) | copy-start | bytes 49156
  27.4 7.0 %copy-start.6 = (bf16[4,64,4,128]{3,2,1,0:T(4,128)(2,1)S(1)}, bf16[4,64,4,128]{3,2,1,0:T(4,128)(2,1)}, u32[]{:S(2)}) copy-start(bf16[4,64,4,128]{3,2,1,0:T(4,128)(2,1)} %reshape.254) | copy-start | bytes 786436
  38.2 5.6 %copy-start.17 = (f32[4,128,128]{2,1,0:T(8,128)S(1)}, f32[4,128,128]{2,1,0:T(8,128)}, u32[]{:S(2)}) copy-start(f32[4,128,128]{2,1,0:T(8,128)} %copy-done.16) | copy-start | bytes 786436
  39.2 12.2 %copy-start.10 = (bf16[4,64,4,128]{3,2,1,0:T(4,128)(2,1)}, bf16[4,64,4,128]{3,2,1,0:T(4,128)(2,1)S(1)}, u32[]{:S(2)}) copy-start(bf16[4,64,4,128]{3,2,1,0:T(4,128)(2,1)S(1)} %broadcast_in_dim_reshape.3) | copy-start | bytes 786436
  48.3 3.2 %copy-start.67 = (bf16[1,4,128,128]{2,3,0,1:T(8,128)(2,1)S(1)}, bf16[1,4,128,128]{2,3,0,1:T(8,128)(2,1)}, u32[]{:S(2)}) copy-start(bf16[1,4,128,128]{2,3,0,1:T(8,128)(2,1)} %bitcast_convert_fusion.5) | copy-start | bytes 393220
  51.5 3.5 %copy-start.65 = (bf16[2,2,64,4,128]{4,3,2,1,0:T(4,128)(2,1)S(1)}, bf16[2,2,64,4,128]{4,3,2,1,0:T(4,128)(2,1)}, u32[]{:S(2)}) copy-start(bf16[2,2,64,4,128]{4,3,2,1,0:T(4,128)(2,1)} %reshape_reshape.16) | copy-start | bytes 786436
  51.5 3.5 %copy-start.5 = (f32[4,4,128,128]{3,2,1,0:T(8,128)S(1)}, f32[4,4,128,128]{3,2,1,0:T(8,128)}, u32[]{:S(2)}) copy-start(f32[4,4,128,128]{3,2,1,0:T(8,128)} %copy-done.4) | copy-start | bytes 3145732
  52.5 20.6 %collective-permute-start = (bf16[7,4,128,128]{2,3,0,1:T(8,128)(2,1)}, bf16[7,4,128,128]{2,3,0,1:T(8,128)(2,1)}, u32[]{:S(2)}, u32[]{:S(2)}) collective-permute-start(bf16[7,4,128,128]{2,3,0,1:T(8,128)(2,1)} %pad_maximum_fusion), channel_id=1, source_target_pairs={{0,4},{4,0},{8,12},{12,8},{16,20},{20,16},{24,28},{28,24},{32,36},... | collective-permute-start | bytes 2752520 | tf_op jit(solution)/shard_map/ppermute | solution.py:17
  55.0 4.9 %copy-start.24 = (bf16[2,1,64,4,128]{4,3,2,1,0:T(4,128)(2,1)}, bf16[2,1,64,4,128]{4,3,2,1,0:T(4,128)(2,1)S(1)}, u32[]{:S(2)}) copy-start(bf16[2,1,64,4,128]{4,3,2,1,0:T(4,128)(2,1)S(1)} %slice.244) | copy-start | bytes 393220
  56.6 5.5 %copy-start.58 = (bf16[1,2,64,4,128]{4,3,2,1,0:T(4,128)(2,1)S(1)}, bf16[1,2,64,4,128]{4,3,2,1,0:T(4,128)(2,1)}, u32[]{:S(2)}) copy-start(bf16[1,2,64,4,128]{4,3,2,1,0:T(4,128)(2,1)} %copy-done.57) | copy-start | bytes 393220
  56.6 5.5 %copy-start.60 = (bf16[1,2,64,4,128]{4,3,2,1,0:T(4,128)(2,1)S(1)}, bf16[1,2,64,4,128]{4,3,2,1,0:T(4,128)(2,1)}, u32[]{:S(2)}) copy-start(bf16[1,2,64,4,128]{4,3,2,1,0:T(4,128)(2,1)} %copy-done.59) | copy-start | bytes 393220
  56.6 5.5 %copy-start.93 = (f32[2,64,4]{1,0,2:T(2,128)S(1)}, f32[2,64,4]{1,0,2:T(2,128)}, u32[]{:S(2)}) copy-start(f32[2,64,4]{1,0,2:T(2,128)} %copy.662) | copy-start | bytes 6148
  62.1 4.6 %copy-start.25 = (bf16[2,1,64,4,128]{4,3,2,1,0:T(4,128)(2,1)S(1)}, bf16[2,1,64,4,128]{4,3,2,1,0:T(4,128)(2,1)}, u32[]{:S(2)}) copy-start(bf16[2,1,64,4,128]{4,3,2,1,0:T(4,128)(2,1)} %copy-done.24) | copy-start | bytes 393220
  62.1 4.6 %copy-start.92 = (f32[2,64,4]{1,2,0:T(4,128)S(1)}, f32[2,64,4]{1,2,0:T(4,128)}, u32[]{:S(2)}) copy-start(f32[2,64,4]{1,2,0:T(4,128)} %slice_bitcast_fusion.11) | copy-start | bytes 6148
  63.5 5.5 %copy-start.91 = (f32[2,64,4]{1,2,0:T(4,128)S(1)}, f32[2,64,4]{1,2,0:T(4,128)}, u32[]{:S(2)}) copy-start(f32[2,64,4]{1,2,0:T(4,128)} %slice_bitcast_fusion.10) | copy-start | bytes 6148
  65.2 3.7 %copy-start.63 = (f32[4,128,128]{1,2,0:S(1)}, f32[4,128,128]{1,2,0}, u32[]{:S(2)}) copy-start(f32[4,128,128]{1,2,0} %fusion.150) | copy-start | bytes 786436
  65.2 3.7 %copy-start.64 = (f32[4,128,128]{1,2,0:S(1)}, f32[4,128,128]{1,2,0}, u32[]{:S(2)}) copy-start(f32[4,128,128]{1,2,0} %fusion.154) | copy-start | bytes 786436
  65.2 4.5 %copy-start.19 = (bf16[4,64,4,128]{3,2,1,0:T(4,128)(2,1)S(1)}, bf16[4,64,4,128]{3,2,1,0:T(4,128)(2,1)}, u32[]{:S(2)}) copy-start(bf16[4,64,4,128]{3,2,1,0:T(4,128)(2,1)} %reshape.252) | copy-start | bytes 786436
  68.9 2.9 %copy-start.11 = (bf16[4,64,4,128]{3,2,1,0:T(4,128)(2,1)S(1)}, bf16[4,64,4,128]{3,2,1,0:T(4,128)(2,1)}, u32[]{:S(2)}) copy-start(bf16[4,64,4,128]{3,2,1,0:T(4,128)(2,1)} %copy-done.10) | copy-start | bytes 786436
  74.6 51.2 %copy-start.9 = (f32[7,4,128,128]{2,3,0,1:T(8,128)}, f32[7,4,128,128]{2,3,0,1:T(8,128)S(1)}, u32[]{:S(2)}) copy-start(f32[7,4,128,128]{2,3,0,1:T(8,128)S(1)} %convert_element_type.323) | copy-start | bytes 5505028
  75.1 18.6 %collective-permute-start.1 = (bf16[6,4,128,128]{2,3,0,1:T(8,128)(2,1)S(1)}, bf16[6,4,128,128]{2,3,0,1:T(8,128)(2,1)S(1)}, u32[]{:S(2)}, u32[]{:S(2)}) collective-permute-start(bf16[6,4,128,128]{2,3,0,1:T(8,128)(2,1)S(1)} %pad_maximum_fusion.1), channel_id=1, source_target_pairs={{0,8},{4,12},{8,0},{12,4},{16,24},{20,28},{24,16},{28,20},{32,40},... | collective-permute-start | bytes 2359304 | tf_op jit(solution)/shard_map/ppermute | solution.py:17
  93.9 31.9 %copy-start.13 = (f32[6,4,128,128]{2,3,0,1:T(8,128)}, f32[6,4,128,128]{2,3,0,1:T(8,128)S(1)}, u32[]{:S(2)}) copy-start(f32[6,4,128,128]{2,3,0,1:T(8,128)S(1)} %convert_element_type.328) | copy-start | bytes 4718596
  94.3 31.4 %collective-permute-start.2 = (bf16[5,4,128,128]{2,3,0,1:T(8,128)(2,1)S(1)}, bf16[5,4,128,128]{2,3,0,1:T(8,128)(2,1)S(1)}, u32[]{:S(2)}, u32[]{:S(2)}) collective-permute-start(bf16[5,4,128,128]{2,3,0,1:T(8,128)(2,1)S(1)} %pad_maximum_fusion.2), channel_id=1, source_target_pairs={{0,16},{4,20},{8,24},{12,28},{16,0},{20,4},{24,8},{28,12},{32,48},... | collective-permute-start | bytes 1966088 | tf_op jit(solution)/shard_map/ppermute | solution.py:17
  125.8 5.8 %copy-start.21 = (f32[5,4,128,128]{2,3,0,1:T(8,128)}, f32[5,4,128,128]{2,3,0,1:T(8,128)S(1)}, u32[]{:S(2)}) copy-start(f32[5,4,128,128]{2,3,0,1:T(8,128)S(1)} %convert_element_type.333) | copy-start | bytes 3932164
  126.1 27.9 %collective-permute-start.3 = (bf16[4,4,128,128]{2,3,0,1:T(8,128)(2,1)S(1)}, bf16[4,4,128,128]{2,3,0,1:T(8,128)(2,1)S(1)}, u32[]{:S(2)}, u32[]{:S(2)}) collective-permute-start(bf16[4,4,128,128]{2,3,0,1:T(8,128)(2,1)S(1)} %pad_maximum_fusion.3), channel_id=1, source_target_pairs={{0,32},{4,36},{8,40},{12,44},{16,48},{20,52},{24,56},{28,60},{32,0... | collective-permute-start | bytes 1572872 | tf_op jit(solution)/shard_map/ppermute | solution.py:17
  131.7 22.6 %copy-start.51 = (bf16[4,128,128]{1,2,0:T(8,128)(2,1)}, bf16[4,128,128]{1,2,0:T(8,128)(2,1)S(1)}, u32[]{:S(2)}) copy-start(bf16[4,128,128]{1,2,0:T(8,128)(2,1)S(1)} %get-tuple-element.27) | copy-start | bytes 393220
  131.7 22.6 %copy-start.52 = (bf16[4,128,128]{1,2,0:T(8,128)(2,1)}, bf16[4,128,128]{1,2,0:T(8,128)(2,1)S(1)}, u32[]{:S(2)}) copy-start(bf16[4,128,128]{1,2,0:T(8,128)(2,1)S(1)} %get-tuple-element.28) | copy-start | bytes 393220
  154.1 9.4 %copy-start.14 = (f32[4,4,128,128]{2,3,0,1:T(8,128)}, f32[4,4,128,128]{2,3,0,1:T(8,128)S(1)}, u32[]{:S(2)}) copy-start(f32[4,4,128,128]{2,3,0,1:T(8,128)S(1)} %convert_element_type.338) | copy-start | bytes 3145732
  154.4 8.9 %collective-permute-start.4 = (bf16[3,4,128,128]{2,3,0,1:T(8,128)(2,1)S(1)}, bf16[3,4,128,128]{2,3,0,1:T(8,128)(2,1)S(1)}, u32[]{:S(2)}, u32[]{:S(2)}) collective-permute-start(bf16[3,4,128,128]{2,3,0,1:T(8,128)(2,1)S(1)} %pad_maximum_fusion.4), channel_id=1, source_target_pairs={{0,64},{4,68},{8,72},{12,76},{16,80},{20,84},{24,88},{28,92},{32,9... | collective-permute-start | bytes 1179656 | tf_op jit(solution)/shard_map/ppermute | solution.py:17
  163.4 4.2 %copy-start.23 = (f32[3,4,128,128]{2,3,0,1:T(8,128)}, f32[3,4,128,128]{2,3,0,1:T(8,128)S(1)}, u32[]{:S(2)}) copy-start(f32[3,4,128,128]{2,3,0,1:T(8,128)S(1)} %convert_element_type.343) | copy-start | bytes 2359300
  163.5 3.7 %copy-start.55 = (bf16[4,128,128]{1,2,0:T(8,128)(2,1)}, bf16[4,128,128]{1,2,0:T(8,128)(2,1)S(1)}, u32[]{:S(2)}) copy-start(bf16[4,128,128]{1,2,0:T(8,128)(2,1)S(1)} %get-tuple-element.18) | copy-start | bytes 393220
  163.5 4.1 %copy-start.53 = (bf16[4,128,128]{1,2,0:T(8,128)(2,1)}, bf16[4,128,128]{1,2,0:T(8,128)(2,1)S(1)}, u32[]{:S(2)}) copy-start(bf16[4,128,128]{1,2,0:T(8,128)(2,1)S(1)} %get-tuple-element.17) | copy-start | bytes 393220
  163.6 7.1 %collective-permute-start.5 = (bf16[2,4,128,128]{2,3,0,1:T(8,128)(2,1)S(1)}, bf16[2,4,128,128]{2,3,0,1:T(8,128)(2,1)S(1)}, u32[]{:S(2)}, u32[]{:S(2)}) collective-permute-start(bf16[2,4,128,128]{2,3,0,1:T(8,128)(2,1)S(1)} %pad_maximum_fusion.5), channel_id=1, source_target_pairs={{0,128},{4,132},{8,136},{12,140},{16,144},{20,148},{24,152},{28,15... | collective-permute-start | bytes 786440 | tf_op jit(solution)/shard_map/ppermute | solution.py:17
  167.2 5.3 %copy-start.7 = (bf16[4,64,4,128]{3,2,1,0:T(4,128)(2,1)S(1)}, bf16[4,64,4,128]{3,2,1,0:T(4,128)(2,1)}, u32[]{:S(2)}) copy-start(bf16[4,64,4,128]{3,2,1,0:T(4,128)(2,1)} %reshape.254) | copy-start | bytes 786436
  167.2 5.3 %copy-start.22 = (f32[2,2,64,4,128]{4,2,3,1,0:T(8,128)S(1)}, f32[2,2,64,4,128]{4,2,3,1,0:T(8,128)}, u32[]{:S(2)}) copy-start(f32[2,2,64,4,128]{4,2,3,1,0:T(8,128)} %concatenate.43.clone) | copy-start | bytes 1572868
  167.2 5.3 %copy-start.27 = (f32[1,2,64,4,128]{4,2,3,1,0:T(8,128)S(1)}, f32[1,2,64,4,128]{4,2,3,1,0:T(8,128)}, u32[]{:S(2)}) copy-start(f32[1,2,64,4,128]{4,2,3,1,0:T(8,128)} %fusion.76) | copy-start | bytes 786436
  167.2 5.3 %copy-start.44 = (f32[4,4,64,128]{3,2,1,0:T(8,128)S(1)}, f32[4,4,64,128]{3,2,1,0:T(8,128)}, u32[]{:S(2)}) copy-start(f32[4,4,64,128]{3,2,1,0:T(8,128)} %fusion.110) | copy-start | bytes 1572868
  167.2 5.3 %copy-start.82 = (f32[4,64,4]{1,2,0:T(4,128)S(1)}, f32[4,64,4]{1,2,0:T(4,128)}, u32[]{:S(2)}) copy-start(f32[4,64,4]{1,2,0:T(4,128)} %get-tuple-element.53) | copy-start | bytes 12292
  167.3 5.3 %copy-start.83 = (f32[4,64,4]{1,2,0:T(4,128)S(1)}, f32[4,64,4]{1,2,0:T(4,128)}, u32[]{:S(2)}) copy-start(f32[4,64,4]{1,2,0:T(4,128)} %get-tuple-element.54) | copy-start | bytes 12292
  167.3 5.3 %copy-start.84 = (f32[4,64,4]{1,2,0:T(4,128)S(1)}, f32[4,64,4]{1,2,0:T(4,128)}, u32[]{:S(2)}) copy-start(f32[4,64,4]{1,2,0:T(4,128)} %get-tuple-element.55) | copy-start | bytes 12292
  167.3 5.3 %copy-start.85 = (f32[4,64,4]{1,2,0:T(4,128)S(1)}, f32[4,64,4]{1,2,0:T(4,128)}, u32[]{:S(2)}) copy-start(f32[4,64,4]{1,2,0:T(4,128)} %get-tuple-element.56) | copy-start | bytes 12292
  167.3 5.3 %copy-start.86 = (f32[4,64,4]{1,2,0:T(4,128)S(1)}, f32[4,64,4]{1,2,0:T(4,128)}, u32[]{:S(2)}) copy-start(f32[4,64,4]{1,2,0:T(4,128)} %get-tuple-element.57) | copy-start | bytes 12292
  167.3 5.3 %copy-start.87 = (f32[4,64,4]{1,2,0:T(4,128)S(1)}, f32[4,64,4]{1,2,0:T(4,128)}, u32[]{:S(2)}) copy-start(f32[4,64,4]{1,2,0:T(4,128)} %get-tuple-element.58) | copy-start | bytes 12292
  167.3 5.3 %copy-start.88 = (f32[4,64,4]{1,2,0:T(4,128)S(1)}, f32[4,64,4]{1,2,0:T(4,128)}, u32[]{:S(2)}) copy-start(f32[4,64,4]{1,2,0:T(4,128)} %get-tuple-element.59) | copy-start | bytes 12292
  167.3 5.3 %copy-start.89 = (f32[4,64,4]{1,2,0:T(4,128)S(1)}, f32[4,64,4]{1,2,0:T(4,128)}, u32[]{:S(2)}) copy-start(f32[4,64,4]{1,2,0:T(4,128)} %get-tuple-element.60) | copy-start | bytes 12292
  167.3 5.3 %copy-start.90 = (f32[4,64,4]{1,2,0:T(4,128)S(1)}, f32[4,64,4]{1,2,0:T(4,128)}, u32[]{:S(2)}) copy-start(f32[4,64,4]{1,2,0:T(4,128)} %get-tuple-element.61) | copy-start | bytes 12292
  178.4 23.2 %all-to-all-start.3 = ((f32[64,16,4]{1,2,0:T(4,128)}), f32[64,16,4]{1,2,0:T(4,128)}, u32[]{:S(2)}, u32[]{:S(2)}) async-start(f32[64,16,4]{1,2,0:T(4,128)} %broadcast_in_dim.14), calls=%async_computation.3 | async-start | bytes 262144 | tf_op jit(solution)/shard_map/all_to_all | solution.py:28
  201.6 19.2 %all-to-all-start.1 = ((bf16[4,256,512]{2,1,0:T(8,128)(2,1)}), bf16[4,256,512]{2,1,0:T(8,128)(2,1)}, u32[]{:S(2)}, u32[]{:S(2)}) async-start(bf16[4,256,512]{2,1,0:T(8,128)(2,1)} %bitcast.606), calls=%async_computation.1 | async-start | bytes 2097152 | tf_op jit(solution)/shard_map/all_to_all | solution.py:44
  220.8 6.6 %copy-start.50 = (bf16[4,128,128]{1,2,0:T(8,128)(2,1)S(1)}, bf16[4,128,128]{1,2,0:T(8,128)(2,1)}, u32[]{:S(2)}) copy-start(bf16[4,128,128]{1,2,0:T(8,128)(2,1)} %copy-done.49) | copy-start | bytes 393220
  220.8 7.7 %copy-start.46 = (bf16[4,128,128]{1,2,0:T(8,128)(2,1)S(1)}, bf16[4,128,128]{1,2,0:T(8,128)(2,1)}, u32[]{:S(2)}) copy-start(bf16[4,128,128]{1,2,0:T(8,128)(2,1)} %copy-done.45) | copy-start | bytes 393220
  220.8 57.8 %all-to-all-start.2 = ((bf16[64,32,512]{2,1,0:T(8,128)(2,1)}), bf16[64,32,512]{2,1,0:T(8,128)(2,1)}, u32[]{:S(2)}, u32[]{:S(2)}) async-start(bf16[64,32,512]{2,1,0:T(8,128)(2,1)} %bitcast.578), calls=%async_computation.2 | async-start | bytes 4194304 | tf_op jit(solution)/shard_map/all_to_all | solution.py:44
  227.4 3.1 %copy-start.54 = (bf16[4,128,128]{1,2,0:T(8,128)(2,1)S(1)}, bf16[4,128,128]{1,2,0:T(8,128)(2,1)}, u32[]{:S(2)}) copy-start(bf16[4,128,128]{1,2,0:T(8,128)(2,1)} %copy-done.53) | copy-start | bytes 393220
  227.4 4.1 %copy-start.41 = (f32[2,4,128,128]{2,3,0,1:T(8,128)S(1)}, f32[2,4,128,128]{2,3,0,1:T(8,128)}, u32[]{:S(2)}) copy-start(f32[2,4,128,128]{2,3,0,1:T(8,128)} %copy-done.40) | copy-start | bytes 1572868
  (42 other events, 76.4 us)
where the time goes:
time: 283 us; the launch traced here: 281 us
  waiting for transfers between devices  116 us (41%)
  matrix products  52.6 us (19%)
  local copies, waits for them, and re-layouts  45.6 us (16%)
  starting transfers between devices  44.4 us (16%)
  other arithmetic  20.6 us (7%)
    ppermute x6, waiting for transfers between devices, partner_2(): return lax.ppermute(value, axis, pairs)  74.6 us
    all_to_all x2, waiting for transfers between devices, sent_and_summed(): lax.all_to_all(tiles, axis, split_axis=0, concat_axis=0, tiled=True)  34 us
    unnamed x28, matrix products  18.9 us
    all_to_all x2, starting transfers between devices, copy_for_each(): lax.all_to_all(jnp.broadcast_to(shard[None], (devices, *shard.shape)), ax...  18.1 us
    ppermute x6, starting transfers between devices, partner_2(): return lax.ppermute(value, axis, pairs)  15.2 us
    all_to_all x2, starting transfers between devices, sent_and_summed(): lax.all_to_all(tiles, axis, split_axis=0, concat_axis=0, tiled=True)  11.1 us
    unnamed x206, local copies, waits for them, and re-layouts  8.72 us
    all_to_all x2, waiting for transfers between devices, copy_for_each(): lax.all_to_all(jnp.broadcast_to(shard[None], (devices, *shard.shape)), ax...  7.3 us
  transfers between devices with their start and end apart: 10, of which 8 were waited for; matrix products, arithmetic and copies ran while one was open for 30% of the time, Pallas kernels for 0%

commit v1 on v0

v1 whole, which is shorter than its diff:
```python
import math

import jax
import jax.numpy as jnp
from jax import lax
from jax.experimental import pallas as pl
from jax.experimental.pallas import tpu as pltpu
from jax.sharding import PartitionSpec as P

SPAN = 64
CODES = 16
NX, NZ = 4, 8
F32, BF16 = jnp.float32, jnp.bfloat16
MESH = pl.DeviceIdType.MESH
NN = (((1,), (0,)), ((), ()))
NT = (((1,), (1,)), ((), ()))
TN = (((0,), (0,)), ((), ()))


def mm(left, right, dims):
    return lax.dot_general(left, right, dims, preferred_element_type=F32)


def remote(src, dst, send_sem, recv_sem, device):
    return pltpu.make_async_remote_copy(
        src_ref=src,
        dst_ref=dst,
        send_sem=send_sem,
        recv_sem=recv_sem,
        device_id=device,
        device_id_type=MESH,
    )


def mod(value, size):
    return lax.rem(value + size, size)


def bit_of(value, index):
    return lax.rem(lax.div(value, 2**index), 2)


def kernel(
    q_ref, k_ref, v_ref, table_ref, code_ref, w_ref, cot_ref,
    mixed_ref, wg_ref, qg_ref, kg_ref, vg_ref, tg_ref,
    cotall, coefb, scores, lw, probs, sgbuf, gbuf, abuf, attnl, qgl, kgl, vgl,
    dsend, drecv, zsend_f, zrecv_f, xsend_f, xrecv_f, rsend_f, rx_f, fall,
    t0send, t0recv, tsend, trecv, zsend_b, zrecv_b, xsend_b, xrecv_b, gsend, gall,
    mpart, mrelay, mrecv, wpart, wrecv, wrelay, wxrecv, wz, wzrecv,
    tgsend, tgcore, tgzsend, tgz, tgxsend, tgx,
    cot_s, cot_r, core_s, core_r, zf_s, zf_r, xf_s, xf_r, rf_s, rf_r,
    zb_s, zb_r, xb_s, xb_r, rb_s, rb_r, m_s, m_r, wc_s, wc_r, wx_s, wx_r, wz_s, wz_r,
    tz_s, tz_r, tx_s, tx_r,
):
    s = lax.axis_index("seq")
    y = lax.axis_index("head")
    c = lax.rem(s, 2)
    z = lax.rem(lax.div(s, 2), NZ)
    x = lax.div(s, 2 * NZ)
    other = 1 - c
    heads, size = 4, 128
    rows = q_ref.shape[0]
    half = rows // 2

    def at_y(target):
        return (s, target)

    def at_z(target):
        return ((x * NZ + target) * 2 + c, y)

    def at_x(target):
        return ((target * NZ + z) * 2 + c, y)

    partner = (s + 1 - 2 * c, y)
    level_bits = [bit_of(z, 0), bit_of(z, 1), bit_of(z, 2), bit_of(x, 0), bit_of(x, 1)]
    pending = []

    def go(copy, cond=None):
        pending.append((copy, cond))
        if cond is None:
            copy.start()
        else:
            pl.when(cond)(lambda: copy.start())

    def arrived(dst, sem, cond=None):
        copy = remote(dst, dst, sem, sem, partner)
        if cond is None:
            copy.wait_recv()
        else:
            pl.when(cond)(lambda: copy.wait_recv())

    def col(h):
        return slice(h * size, (h + 1) * size)

    barrier = pltpu.get_barrier_semaphore()
    partners = [partner]
    partners += [at_y(mod(y + off, 4)) for off in range(1, 4)]
    partners += [at_z(mod(z + off, NZ)) for off in range(1, NZ)]
    partners += [at_x(mod(x + off, NX)) for off in range(1, NX)]
    for device in partners:
        pl.semaphore_signal(barrier, inc=1, device_id=device, device_id_type=MESH)

    for h in range(heads):
        dsend[col(h), :] = mm(k_ref[:, col(h)], v_ref[:, col(h)], TN).astype(BF16)
    for l in range(5):
        @pl.when(level_bits[l] == 0)
        def _(l=l):
            fall[l, c] = jnp.zeros((256, size), BF16)
    cotall[y] = cot_ref[...]
    pl.semaphore_wait(barrier, len(partners))

    right, left = mod(y + 1, 4), mod(y - 1, 4)
    top, low = pl.ds(0, half), pl.ds(half, half)
    go(remote(cot_ref.at[top], cotall.at[y, top], cot_s.at[0], cot_r.at[0], at_y(right)))
    go(remote(cot_ref.at[low], cotall.at[y, low], cot_s.at[2], cot_r.at[2], at_y(left)))
    go(remote(cot_ref.at[low], cotall.at[y, low], cot_s.at[1], cot_r.at[1], at_y(right)))
    go(remote(cot_ref.at[top], cotall.at[y, top], cot_s.at[3], cot_r.at[3], at_y(left)))
    go(remote(dsend, drecv, core_s.at[0], core_r.at[0], partner))

    code = code_ref[...]
    levels = code.shape[1]
    lane = lax.broadcasted_iota(jnp.int32, (1, levels), 1)
    scale = jnp.zeros((1, levels), F32)
    scales = [1.0 / math.sqrt(SPAN * 2 ** max(l - 1, 0)) for l in range(levels)]
    for l in range(levels):
        scale = jnp.where(lane == l, scales[l], scale)
    coefs = []
    for h in range(heads):
        lam = jnp.zeros((rows, levels), F32)
        for entry in range(CODES):
            lam = jnp.where(code == entry, table_ref[entry, h], lam)
        coefs.append(lam * scale)

    arrived(drecv, core_r.at[0])
    half_rows = pl.ds(pl.multiple_of(c * 256, 256), 256)
    zsend_f[...] = (dsend[half_rows, :].astype(F32) + drecv[half_rows, :].astype(F32)).astype(BF16)
    for off in range(1, NZ):
        zt = mod(z + off, NZ)
        go(remote(zsend_f.at[pl.ds(pl.multiple_of(zt * 32, 32), 32)], zrecv_f.at[z],
                  zf_s.at[off], zf_r.at[off], at_z(zt)))
    own_slice = pl.ds(pl.multiple_of(z * 32, 32), 32)
    zrecv_f[z] = zsend_f[own_slice, :]

    for h in range(heads):
        for l in range(3, levels):
            coefb[h, l - 3] = jnp.broadcast_to(coefs[h][:, l:l + 1], (rows, size))

    arrived(cotall.at[left, top], cot_r.at[0])
    go(remote(cotall.at[left, top], cotall.at[left, top], cot_s.at[4], cot_r.at[4], at_y(right)))
    arrived(cotall.at[right, low], cot_r.at[2])
    go(remote(cotall.at[right, low], cotall.at[right, low], cot_s.at[5], cot_r.at[5], at_y(left)))

    for off in range(1, NZ):
        arrived(zrecv_f.at[mod(z - off, NZ)], zf_r.at[off])
    parts = [zrecv_f[i].astype(F32) for i in range(NZ)]
    pairs = [parts[2 * i] + parts[2 * i + 1] for i in range(4)]
    quads = [pairs[0] + pairs[1], pairs[2] + pairs[3]]
    xsend_f[...] = (quads[0] + quads[1]).astype(BF16)
    for off in range(1, NX):
        xt = mod(x + off, NX)
        go(remote(xsend_f, xrecv_f.at[x], xf_s.at[off], xf_r.at[off], at_x(xt)), xt > x)
    for zt in range(NZ):
        if zt & 1:
            rsend_f[zt, 0] = parts[zt - 1].astype(BF16)
        if zt & 2:
            rsend_f[zt, 1] = pairs[2 * (zt // 4)].astype(BF16)
        if zt & 4:
            rsend_f[zt, 2] = quads[0].astype(BF16)
    for off in range(1, NZ):
        zt = mod(z + off, NZ)
        for l in range(3):
            go(remote(rsend_f.at[zt, l], fall.at[l, c, own_slice],
                      rf_s.at[off, l], rf_r.at[off, l], at_z(zt)), bit_of(zt, l) == 1)
    for l in range(3):
        @pl.when(level_bits[l] == 1)
        def _(l=l):
            fall[l, c, own_slice, :] = rsend_f[z, l]

    row = lax.broadcasted_iota(jnp.int32, (rows, rows), 0)
    column = lax.broadcasted_iota(jnp.int32, (rows, rows), 1)
    row_span, column_span = row // SPAN, column // SPAN
    in_level = [
        (row_span == column_span) & (column <= row),
        (row_span // 2 == column_span // 2) & (column_span < row_span),
        (row_span >= 2) & (column_span < 2),
    ]
    for h in range(heads):
        weight = jnp.zeros((rows, rows), F32)
        for l in range(3):
            weight = jnp.where(in_level[l], coefs[h][:, l:l + 1], weight)
        score = mm(q_ref[:, col(h)], k_ref[:, col(h)], NT)
        scores[h] = score
        lw[h] = weight
        prob = (score * weight).astype(BF16)
        probs[h] = prob
        attnl[:, col(h)] = mm(prob, v_ref[:, col(h)], NN)

    for off in range(1, NX):
        xs = mod(x - off, NX)
        arrived(xrecv_f.at[xs], xf_r.at[off], xs < x)

    @pl.when(bit_of(x, 0) == 1)
    def _():
        rx_f[0] = xrecv_f[x - 1]
        fall[3, c, own_slice, :] = xrecv_f[x - 1]

    @pl.when(x >= 2)
    def _():
        both = (xrecv_f[0].astype(F32) + xrecv_f[1].astype(F32)).astype(BF16)
        rx_f[1] = both
        fall[4, c, own_slice, :] = both

    for off in range(1, NZ):
        zt = mod(z + off, NZ)
        for l in range(3, 5):
            go(remote(rx_f.at[l - 3], fall.at[l, c, own_slice],
                      rf_s.at[off, l], rf_r.at[off, l], at_z(zt)), level_bits[l] == 1)

    opposite = mod(y + 2, 4)
    arrived(cotall.at[left, low], cot_r.at[1])
    arrived(cotall.at[right, top], cot_r.at[3])
    arrived(cotall.at[opposite, top], cot_r.at[4])
    arrived(cotall.at[opposite, low], cot_r.at[5])
    full_rows = jnp.concatenate([cotall[i] for i in range(4)], axis=1)
    gbuf[...] = mm(full_rows, w_ref[...], NT).astype(BF16)

    for h in range(heads):
        grad = gbuf[:, col(h)].astype(F32)
        for l in range(6):
            sgbuf[h, :, col(l)] = (coefb[h, l] * grad).astype(BF16)
        terms = mm(q_ref[:, col(h)], sgbuf[h], TN)
        t0send[col(h), :] = terms[:, col(0)].astype(BF16)
        for l in range(5):
            tsend[l, h // 2, col(h % 2), :] = terms[:, col(l + 1)].astype(BF16)
    go(remote(tsend.at[:, other], trecv, core_s.at[1], core_r.at[1], partner))
    go(remote(t0send, t0recv, core_s.at[2], core_r.at[2], partner))

    code_f = code.astype(F32)
    wide = jnp.concatenate([code_f, jnp.zeros((rows, size - levels), F32)], axis=1)
    code_t = wide.T
    entry_row = lax.broadcasted_iota(jnp.int32, (CODES, rows), 0).astype(F32)
    one_hot = [
        jnp.where(jnp.broadcast_to(code_t[l:l + 1, :], (CODES, rows)) == entry_row, 1.0, 0.0).astype(BF16)
        for l in range(levels)
    ]
    table_parts = []

    def local_back(h):
        grad = gbuf[:, col(h)]
        prob_grad = mm(grad, v_ref[:, col(h)], NT)
        score_grad = (prob_grad * lw[h]).astype(BF16)
        product = scores[h] * prob_grad
        total = jnp.zeros((CODES, rows), F32)
        for l in range(3):
            masked = jnp.where(in_level[l], product, 0.0).astype(BF16)
            total = total + scales[l] * mm(one_hot[l], masked, NN)
        table_parts.append(total[:, :size] + total[:, size:])
        qgl[:, col(h)] = mm(score_grad, k_ref[:, col(h)], NN)
        kgl[:, col(h)] = mm(score_grad, q_ref[:, col(h)], TN)
        vgl[:, col(h)] = mm(probs[h], grad, TN)

    for h in range(2):
        local_back(h)

    arrived(trecv, core_r.at[1])
    for l in range(5):
        zsend_b[l] = (tsend[l, c].astype(F32) + trecv[l].astype(F32)).astype(BF16)
    for off in range(1, NZ):
        zt = mod(z + off, NZ)
        for l in range(5):
            go(remote(zsend_b.at[l, pl.ds(pl.multiple_of(zt * 32, 32), 32)], zrecv_b.at[z, l],
                      zb_s.at[off, l], zb_r.at[off, l], at_z(zt)), level_bits[l] == 1)
    for l in range(5):
        @pl.when(level_bits[l] == 1)
        def _(l=l):
            zrecv_b[z, l] = zsend_b[l, own_slice, :]

    for off in range(1, NZ):
        zs = mod(z - off, NZ)
        zs_slice = pl.ds(pl.multiple_of(zs * 32, 32), 32)
        for l in range(5):
            arrived(fall.at[l, c, zs_slice], rf_r.at[off, l], level_bits[l] == 1)
    go(remote(fall.at[:, c], fall.at[:, c], core_s.at[3], core_r.at[3], partner))

    for h in range(2, heads):
        local_back(h)

    arrived(fall.at[:, other], core_r.at[3])

    for h in range(heads):
        query, grad = q_ref[:, col(h)], gbuf[:, col(h)].astype(F32)
        found = [jnp.where(c == 1, drecv[col(h), :], jnp.zeros((size, size), BF16))]
        found += [fall[l, h // 2, col(h % 2), :] for l in range(5)]
        found = jnp.concatenate(found, axis=1)
        reads = mm(query, found, NN)
        attention = attnl[:, col(h)]
        total = table_parts[h]
        for l in range(6):
            read = reads[:, col(l)]
            attention = attention + coefb[h, l] * read
            total = total + scales[l + 3] * mm(one_hot[l + 3], (grad * read).astype(BF16), NN)
        table_parts[h] = total
        abuf[:, col(h)] = attention.astype(BF16)
        qg_ref[:, col(h)] = (qgl[:, col(h)] + mm(sgbuf[h], found, NT)).astype(BF16)

    def product_for(target):
        columns = pl.ds(pl.multiple_of(target * 512, 512), 512)
        mpart[target] = mm(abuf[...], w_ref[:, columns], NN).astype(BF16)

    product_for(opposite)
    go(remote(mpart.at[opposite, top], mrelay.at[0], m_s.at[0], m_r.at[0], at_y(left)))
    go(remote(mpart.at[opposite, low], mrelay.at[1], m_s.at[1], m_r.at[1], at_y(right)))

    x_right, x_left, x_opposite = mod(x + 1, 4), mod(x - 1, 4), mod(x + 2, 4)

    def weight_part(step, target):
        part = mm(cotall[target], abuf[...], TN)
        for block in range(16):
            wpart[target, block % 2, pl.ds((block // 2) * 32, 32), :] = (
                part[block * 32:(block + 1) * 32].astype(BF16)
            )
        go(remote(wpart.at[target, other], wrecv.at[target], wc_s.at[step], wc_r.at[step], partner))

    weight_part(0, x_opposite)
    product_for(left)
    product_for(right)
    weight_part(1, x_left)

    def weight_chip(step, target):
        arrived(wrecv.at[target], wc_r.at[step])
        wpart[target, c] = (wpart[target, c].astype(F32) + wrecv[target].astype(F32)).astype(BF16)

    weight_chip(0, x_opposite)
    go(remote(wpart.at[x_opposite, c, top], wrelay.at[0], wx_s.at[0], wx_r.at[0], at_x(x_left)))
    go(remote(wpart.at[x_opposite, c, low], wrelay.at[1], wx_s.at[1], wx_r.at[1], at_x(x_right)))

    arrived(mrelay.at[0], m_r.at[0])
    mpart[left, top] = (mpart[left, top].astype(F32) + mrelay[0].astype(F32)).astype(BF16)
    go(remote(mpart.at[left], mrecv.at[0], m_s.at[2], m_r.at[2], at_y(left)))
    arrived(mrelay.at[1], m_r.at[1])
    mpart[right, low] = (mpart[right, low].astype(F32) + mrelay[1].astype(F32)).astype(BF16)
    go(remote(mpart.at[right], mrecv.at[1], m_s.at[3], m_r.at[3], at_y(right)))

    weight_part(2, x_right)
    weight_part(3, x)
    product_for(y)

    lane128 = lax.broadcasted_iota(jnp.int32, (CODES, size), 1)
    partial_table = jnp.zeros((CODES, size), F32)
    for h in range(heads):
        summed = jnp.sum(table_parts[h], axis=1, keepdims=True)
        partial_table = jnp.where(lane128 == h, summed, partial_table)
    tgsend[...] = partial_table
    go(remote(tgsend, tgcore, core_s.at[4], core_r.at[4], partner))

    for off in range(1, NZ):
        zs = mod(z - off, NZ)
        for l in range(5):
            bit = bit_of(zs, l) if l < 3 else level_bits[l]
            arrived(zrecv_b.at[zs, l], zb_r.at[off, l], bit == 1)
    for l in range(2):
        @pl.when(level_bits[3 + l] == 1)
        def _(l=l):
            ring = zrecv_b[0, 3 + l].astype(F32)
            for zs in range(1, NZ):
                ring = ring + zrecv_b[zs, 3 + l].astype(F32)
            xsend_b[l] = ring.astype(BF16)
    for off in range(1, NX):
        xt = mod(x + off, NX)
        bit = jnp.where(lax.div(x, 2) == lax.div(xt, 2), 0, 1)
        go(remote(xsend_b.at[bit], xrecv_b.at[x], xb_s.at[off], xb_r.at[off], at_x(xt)), xt < x)

    weight_chip(1, x_left)
    weight_chip(2, x_right)
    arrived(wrelay.at[0], wx_r.at[0])
    wpart[x_left, c, top] = (wpart[x_left, c, top].astype(F32) + wrelay[0].astype(F32)).astype(BF16)
    go(remote(wpart.at[x_left, c], wxrecv.at[0], wx_s.at[2], wx_r.at[2], at_x(x_left)))
    arrived(wrelay.at[1], wx_r.at[1])
    wpart[x_right, c, low] = (wpart[x_right, c, low].astype(F32) + wrelay[1].astype(F32)).astype(BF16)
    go(remote(wpart.at[x_right, c], wxrecv.at[1], wx_s.at[3], wx_r.at[3], at_x(x_right)))

    arrived(tgcore, core_r.at[4])
    tgzsend[...] = tgsend[...] + tgcore[...]
    for off in range(1, NZ):
        go(remote(tgzsend, tgz.at[z], tz_s.at[off], tz_r.at[off], at_z(mod(z + off, NZ))))
    tgz[z] = tgzsend[...]

    for off in range(1, NX):
        xs = mod(x - off, NX)
        arrived(xrecv_b.at[xs], xb_r.at[off], xs > x)
    from_x = jnp.zeros((32, size), F32)
    for xs in range(1, NX):
        from_x = from_x + jnp.where(x < xs, xrecv_b[xs].astype(F32), 0.0)
    quad = zrecv_b[4, 2].astype(F32)
    for zs in range(5, NZ):
        quad = quad + zrecv_b[zs, 2].astype(F32)
    for zt in range(NZ):
        total = from_x
        if zt & 1 == 0:
            total = total + zrecv_b[zt + 1, 0].astype(F32)
        if zt & 2 == 0:
            upper = (zt // 4) * 4 + 2
            total = total + zrecv_b[upper, 1].astype(F32) + zrecv_b[upper + 1, 1].astype(F32)
        if zt & 4 == 0:
            total = total + quad
        gsend[zt] = total.astype(BF16)
    for off in range(1, NZ):
        zt = mod(z + off, NZ)
        go(remote(gsend.at[zt], gall.at[c, own_slice], rb_s.at[off], rb_r.at[off], at_z(zt)))
    gall[c, own_slice, :] = gsend[z]

    weight_chip(3, x)

    for off in range(1, NZ):
        zs = mod(z - off, NZ)
        arrived(gall.at[c, pl.ds(pl.multiple_of(zs * 32, 32), 32)], rb_r.at[off])
    go(remote(gall.at[c], gall.at[c], core_s.at[5], core_r.at[5], partner))

    arrived(wxrecv.at[0], wx_r.at[2])
    arrived(wxrecv.at[1], wx_r.at[3])
    wz[...] = (
        wpart[x, c].astype(F32) + wxrecv[0].astype(F32) + wxrecv[1].astype(F32)
    ).astype(BF16)
    for off in range(1, NZ):
        zt = mod(z + off, NZ)
        go(remote(wz.at[pl.ds(pl.multiple_of(zt * 32, 32), 32)], wzrecv.at[z],
                  wz_s.at[off], wz_r.at[off], at_z(zt)))
    wzrecv[z] = wz[own_slice, :]

    for off in range(1, NZ):
        arrived(tgz.at[mod(z - off, NZ)], tz_r.at[off])
    ring_table = tgz[0]
    for zs in range(1, NZ):
        ring_table = ring_table + tgz[zs]
    tgxsend[...] = ring_table
    for off in range(1, NX):
        go(remote(tgxsend, tgx.at[x], tx_s.at[off], tx_r.at[off], at_x(mod(x + off, NX))))
    tgx[x] = ring_table

    arrived(gall.at[other], core_r.at[5])
    arrived(t0recv, core_r.at[2])
    for h in range(heads):
        back = gall[h // 2, col(h % 2), :].astype(F32) + jnp.where(c == 0, t0recv[col(h), :].astype(F32), 0.0)
        back = back.astype(BF16)
        kg_ref[:, col(h)] = (kgl[:, col(h)] + mm(v_ref[:, col(h)], back, NT)).astype(BF16)
        vg_ref[:, col(h)] = (vgl[:, col(h)] + mm(k_ref[:, col(h)], back, NN)).astype(BF16)

    arrived(mrecv.at[0], m_r.at[2])
    arrived(mrecv.at[1], m_r.at[3])
    mixed_ref[...] = (
        mpart[y].astype(F32) + mrecv[0].astype(F32) + mrecv[1].astype(F32)
    ).astype(BF16)

    for off in range(1, NX):
        arrived(tgx.at[mod(x - off, NX)], tx_r.at[off])
    table = tgx[0]
    for xs in range(1, NX):
        table = table + tgx[xs]
    tokens = rows * 2 * NZ * NX
    tg_ref[...] = table[:, :heads] * (1.0 / math.sqrt(tokens * levels))

    for off in range(1, NZ):
        arrived(wzrecv.at[mod(z - off, NZ)], wz_r.at[off])
    weight = wzrecv[0].astype(F32)
    for zs in range(1, NZ):
        weight = weight + wzrecv[zs].astype(F32)
    wg_ref[...] = weight * (1.0 / math.sqrt(tokens))

    for copy, cond in pending:
        if cond is None:
            copy.wait_send()
        else:
            pl.when(cond)(lambda copy=copy: copy.wait_send())


def per_device(queries, keys, values, level_table, level_code, out_weight, cotangent):
    rows, width = queries.shape
    vmem = pl.BlockSpec(memory_space=pltpu.VMEM)
    smem = pl.BlockSpec(memory_space=pltpu.SMEM)
    dma = pltpu.SemaphoreType.DMA

    def bf(*shape):
        return pltpu.VMEM(shape, BF16)

    def f32(*shape):
        return pltpu.VMEM(shape, F32)

    scratch = [
        bf(4, rows, 512), f32(4, 6, rows, 128), f32(4, rows, rows), f32(4, rows, rows),
        bf(4, rows, rows), bf(4, rows, 768), bf(rows, 512), bf(rows, 512),
        f32(rows, 512), f32(rows, 512), f32(rows, 512), f32(rows, 512),
        bf(512, 128), bf(512, 128), bf(256, 128), bf(NZ, 32, 128), bf(32, 128), bf(NX, 32, 128),
        bf(NZ, 3, 32, 128), bf(2, 32, 128), bf(5, 2, 256, 128),
        bf(512, 128), bf(512, 128), bf(5, 2, 256, 128), bf(5, 256, 128), bf(5, 256, 128),
        bf(NZ, 5, 32, 128), bf(2, 32, 128), bf(NX, 32, 128), bf(NZ, 32, 128), bf(2, 256, 128),
        bf(4, rows, 512), bf(2, rows // 2, 512), bf(2, rows, 512),
        bf(4, 2, 256, 512), bf(4, 256, 512), bf(2, 128, 512), bf(2, 256, 512), bf(256, 512),
        bf(NZ, 32, 512),
        f32(CODES, 128), f32(CODES, 128), f32(CODES, 128), f32(NZ, CODES, 128),
        f32(CODES, 128), f32(NX, CODES, 128),
        dma((6,)), dma((6,)), dma((6,)), dma((6,)), dma((NZ,)), dma((NZ,)), dma((NX,)), dma((NX,)),
        dma((NZ, 5)), dma((NZ, 5)), dma((NZ, 5)), dma((NZ, 5)), dma((NX,)), dma((NX,)),
        dma((NZ,)), dma((NZ,)), dma((4,)), dma((4,)), dma((4,)), dma((4,)), dma((4,)), dma((4,)),
        dma((NZ,)), dma((NZ,)), dma((NZ,)), dma((NZ,)), dma((NX,)), dma((NX,)),
    ]
    shape = jax.ShapeDtypeStruct
    return pl.pallas_call(
        kernel,
        out_shape=(
            shape((rows, width), BF16),
            shape((32, width), F32),
            shape((rows, width), BF16),
            shape((rows, width), BF16),
            shape((rows, width), BF16),
            shape((CODES, 4), F32),
        ),
        in_specs=[vmem, vmem, vmem, smem, vmem, vmem, vmem],
        out_specs=[vmem] * 6,
        scratch_shapes=scratch,
        compiler_params=pltpu.CompilerParams(
            collective_id=0, has_side_effects=True, vmem_limit_bytes=56 * 2**20
        ),
        name="layer",
    )(queries, keys, values, level_table, level_code, out_weight, cotangent)


def solution(mesh):
    wide = P("seq", "head")
    return jax.shard_map(
        per_device,
        mesh=mesh,
        in_specs=(wide, wide, wide, P(None, "head"), P("seq", None), P("head", None), wide),
        out_specs=(wide, wide, wide, wide, wide, P(None, "head")),
        check_vma=False,
    )
```

time: 283 us -> 71 us (0.25)
  waiting for transfers between devices: 116 us -> 0 us
  Pallas kernels: 0 us -> 57.6 us
  matrix products: 52.6 us -> 0 us
  starting transfers between devices: 44.4 us -> 0 us
  local copies, waits for them, and re-layouts: 45.6 us -> 12.3 us
  other arithmetic: 20.6 us -> 0 us
    ppermute x6 -> x0, waiting for transfers between devices: 74.6 us -> none  [partner_2(): return lax.ppermute(value, axis, pairs)]
    pallas_call x0 -> x1, Pallas kernels: none -> 57.6 us  [per_device(): pl.pallas_call(kernel, out_shape=(shape((rows, width), BF16), shape((32,...]
    all_to_all x4 -> x0, waiting for transfers between devices: 41.3 us -> none  [the longest x2 34 us: sent_and_summed(): lax.all_to_all(tiles, axis, split_axis=0, concat_axis=0, tiled=True)]
    dot_general x30 -> x0, matrix products: 33.6 us -> none  [the longest x5 7.18 us: split_einsum(): jnp.einsum(form, left, rest, preferred_element_type=jnp.float32)]
    all_to_all x4 -> x0, starting transfers between devices: 29.2 us -> none  [the longest x2 18.1 us: copy_for_each(): lax.all_to_all(jnp.broadcast_to(shard[None], (devices, *shard.shape)), ax...]
    unnamed x28 -> x0, matrix products: 18.9 us -> none
    ppermute x6 -> x0, starting transfers between devices: 15.2 us -> none  [partner_2(): return lax.ppermute(value, axis, pairs)]
    reduce_sum x5 -> x0, other arithmetic: 7.7 us -> none  [the longest x2 4.7 us: sent_and_summed(): return arrived.astype(jnp.float32).sum(axis=0)]
  transfers between devices with their start and end apart: 10 -> 0, of which waited for: 8 -> 0; matrix products, arithmetic and copies ran while one was open for 30% -> 0% of each run, Pallas kernels for 0% -> 0%
where the time goes in v1:
time: 71 us; the launch traced here: 70.6 us
  Pallas kernels  57.6 us (81%)
  local copies, waits for them, and re-layouts  12.3 us (17%)
    pallas_call x1, Pallas kernels, per_device(): pl.pallas_call(kernel, out_shape=(shape((rows, width), BF16), shape((32,...  57.6 us
    unnamed x7, local copies, waits for them, and re-layouts  11 us

profile of v1, /device:TPU:1, one launch (start us, length us, event | category | flops | bytes accessed | tf_op | source)
XLA Modules:
  0.0 70.6 jit_solution(2966548828623351520)
XLA Ops:
  0.6 1.4 %copy.13.table_ref = f32[16,4]{1,0:T(8,128)} copy(f32[16,4]{0,1:T(4,128)} %param.10) | data formatting | bytes 512 | tf_op args[3]
  2.0 1.5 %copy.14.code_ref = s32[256,9]{1,0:T(8,128)} copy(s32[256,9]{0,1:T(8,128)} %param.11) | data formatting | bytes 18432 | tf_op args[4]
  3.5 57.6 %layer.1 = (bf16[256,512]{1,0:T(8,128)(2,1)}, f32[32,512]{1,0:T(8,128)}, bf16[256,512]{1,0:T(8,128)(2,1)}, bf16[256,512]{1,0:T(8,128)(2,1)}, bf16[256,512]{1,0:T(8,128)(2,1)}, /*index=5*/f32[16,4]{1,0:T(8,128)}) custom-call(bf16[256,512]{1,0:T(8,128)(2,1)} %q_ref.1, bf16[256,512]{1,0:T(8,128)(2,1)} %k_ref.1, bf16[256,512]{1,0:T(8,128)(2,1)} %v_ref.1, ...), custom_call_target="tpu_custom_call" | custom-call | tf_op jit(solution)/shard_map/layer/pallas_call | solution.py:507
  61.1 1.3 %copy.15 = f32[16,4]{0,1:T(4,128)} copy(f32[16,4]{1,0:T(8,128)} %get-tuple-element.11) | data formatting | bytes 512 | tf_op jit(solution)/shard_map/layer/pallas_call | solution.py:507
  62.5 1.7 %copy.21 = bf16[256,512]{1,0:T(8,128)(2,1)} copy(bf16[256,512]{1,0:T(8,128)(2,1)} %get-tuple-element.18) | data formatting | bytes 524288
  64.1 1.5 %copy.22 = f32[32,512]{1,0:T(8,128)} copy(f32[32,512]{1,0:T(8,128)} %get-tuple-element.19) | data formatting | bytes 131072
  65.6 1.7 %copy.23 = bf16[256,512]{1,0:T(8,128)(2,1)} copy(bf16[256,512]{1,0:T(8,128)(2,1)} %get-tuple-element.20) | data formatting | bytes 524288
  67.3 1.7 %copy.24 = bf16[256,512]{1,0:T(8,128)(2,1)} copy(bf16[256,512]{1,0:T(8,128)(2,1)} %get-tuple-element.21) | data formatting | bytes 524288
  68.9 1.7 %copy.25 = bf16[256,512]{1,0:T(8,128)(2,1)} copy(bf16[256,512]{1,0:T(8,128)(2,1)} %get-tuple-element.22) | data formatting | bytes 524288

commit v2 on v1

--- a/solution.py
+++ b/solution.py
@@ -41,9 +41,9 @@
 
 
 def kernel(
-    q_ref, k_ref, v_ref, table_ref, code_ref, w_ref, cot_ref,
+    q_hbm, k_hbm, v_hbm, table_ref, code_ref, w_hbm, cot_hbm,
     mixed_ref, wg_ref, qg_ref, kg_ref, vg_ref, tg_ref,
-    cotall, coefb, scores, lw, probs, sgbuf, gbuf, abuf, attnl, qgl, kgl, vgl,
+    q_ref, k_ref, v_ref, w_ref, load_sems, cotall, coefb, scores, lw, probs, sgbuf, gbuf, abuf, attnl, qgl, kgl, vgl,
     dsend, drecv, zsend_f, zrecv_f, xsend_f, xrecv_f, rsend_f, rx_f, fall,
     t0send, t0recv, tsend, trecv, zsend_b, zrecv_b, xsend_b, xrecv_b, gsend, gall,
     mpart, mrelay, mrecv, wpart, wrecv, wrelay, wxrecv, wz, wzrecv,
@@ -60,6 +60,14 @@
     other = 1 - c
     heads, size = 4, 128
     rows = q_ref.shape[0]
+    loads = [
+        pltpu.make_async_copy(source, target, load_sems.at[i])
+        for i, (source, target) in enumerate(
+            [(cot_hbm, cotall.at[y]), (k_hbm, k_ref), (v_hbm, v_ref), (q_hbm, q_ref), (w_hbm, w_ref)]
+        )
+    ]
+    for load in loads:
+        load.start()
     half = rows // 2
 
     def at_y(target):
@@ -100,35 +108,39 @@
     for device in partners:
         pl.semaphore_signal(barrier, inc=1, device_id=device, device_id_type=MESH)
 
+    loads[1].wait()
+    loads[2].wait()
     for h in range(heads):
         dsend[col(h), :] = mm(k_ref[:, col(h)], v_ref[:, col(h)], TN).astype(BF16)
     for l in range(5):
         @pl.when(level_bits[l] == 0)
         def _(l=l):
             fall[l, c] = jnp.zeros((256, size), BF16)
-    cotall[y] = cot_ref[...]
+    loads[0].wait()
     pl.semaphore_wait(barrier, len(partners))
 
     right, left = mod(y + 1, 4), mod(y - 1, 4)
     top, low = pl.ds(0, half), pl.ds(half, half)
-    go(remote(cot_ref.at[top], cotall.at[y, top], cot_s.at[0], cot_r.at[0], at_y(right)))
-    go(remote(cot_ref.at[low], cotall.at[y, low], cot_s.at[2], cot_r.at[2], at_y(left)))
-    go(remote(cot_ref.at[low], cotall.at[y, low], cot_s.at[1], cot_r.at[1], at_y(right)))
-    go(remote(cot_ref.at[top], cotall.at[y, top], cot_s.at[3], cot_r.at[3], at_y(left)))
+    go(remote(cotall.at[y, top], cotall.at[y, top], cot_s.at[0], cot_r.at[0], at_y(right)))
+    go(remote(cotall.at[y, low], cotall.at[y, low], cot_s.at[2], cot_r.at[2], at_y(left)))
+    go(remote(cotall.at[y, low], cotall.at[y, low], cot_s.at[1], cot_r.at[1], at_y(right)))
+    go(remote(cotall.at[y, top], cotall.at[y, top], cot_s.at[3], cot_r.at[3], at_y(left)))
     go(remote(dsend, drecv, core_s.at[0], core_r.at[0], partner))
 
-    code = code_ref[...]
-    levels = code.shape[1]
-    lane = lax.broadcasted_iota(jnp.int32, (1, levels), 1)
-    scale = jnp.zeros((1, levels), F32)
+    levels = code_ref.shape[0]
+    code_t = code_ref[...].astype(F32)
+    padding = jnp.zeros((size - levels, rows), F32)
+    code = jnp.concatenate([code_t, padding], axis=0).T
+    lane = lax.broadcasted_iota(jnp.int32, (1, size), 1)
+    scale = jnp.zeros((1, size), F32)
     scales = [1.0 / math.sqrt(SPAN * 2 ** max(l - 1, 0)) for l in range(levels)]
     for l in range(levels):
         scale = jnp.where(lane == l, scales[l], scale)
     coefs = []
     for h in range(heads):
-        lam = jnp.zeros((rows, levels), F32)
+        lam = jnp.zeros((rows, size), F32)
         for entry in range(CODES):
-            lam = jnp.where(code == entry, table_ref[entry, h], lam)
+            lam = jnp.where(code == float(entry), table_ref[h, entry], lam)
         coefs.append(lam * scale)
 
     arrived(drecv, core_r.at[0])
@@ -176,6 +188,7 @@
         def _(l=l):
             fall[l, c, own_slice, :] = rsend_f[z, l]
 
+    loads[3].wait()
     row = lax.broadcasted_iota(jnp.int32, (rows, rows), 0)
     column = lax.broadcasted_iota(jnp.int32, (rows, rows), 1)
     row_span, column_span = row // SPAN, column // SPAN
@@ -216,6 +229,7 @@
             go(remote(rx_f.at[l - 3], fall.at[l, c, own_slice],
                       rf_s.at[off, l], rf_r.at[off, l], at_z(zt)), level_bits[l] == 1)
 
+    loads[4].wait()
     opposite = mod(y + 2, 4)
     arrived(cotall.at[left, low], cot_r.at[1])
     arrived(cotall.at[right, top], cot_r.at[3])
@@ -235,9 +249,6 @@
     go(remote(tsend.at[:, other], trecv, core_s.at[1], core_r.at[1], partner))
     go(remote(t0send, t0recv, core_s.at[2], core_r.at[2], partner))
 
-    code_f = code.astype(F32)
-    wide = jnp.concatenate([code_f, jnp.zeros((rows, size - levels), F32)], axis=1)
-    code_t = wide.T
     entry_row = lax.broadcasted_iota(jnp.int32, (CODES, rows), 0).astype(F32)
     one_hot = [
         jnp.where(jnp.broadcast_to(code_t[l:l + 1, :], (CODES, rows)) == entry_row, 1.0, 0.0).astype(BF16)
@@ -457,7 +468,8 @@
     for xs in range(1, NX):
         table = table + tgx[xs]
     tokens = rows * 2 * NZ * NX
-    tg_ref[...] = table[:, :heads] * (1.0 / math.sqrt(tokens * levels))
+    square = jnp.concatenate([table, jnp.zeros((size - CODES, size), F32)], axis=0)
+    tg_ref[...] = square.T[:heads, :CODES] * (1.0 / math.sqrt(tokens * levels))
 
     for off in range(1, NZ):
         arrived(wzrecv.at[mod(z - off, NZ)], wz_r.at[off])
@@ -473,9 +485,22 @@
             pl.when(cond)(lambda copy=copy: copy.wait_send())
 
 
+def store(*refs):
+    sources, targets, sems = refs[:6], refs[6:12], refs[12]
+    copies = [
+        pltpu.make_async_copy(source, target, sems.at[i])
+        for i, (source, target) in enumerate(zip(sources, targets))
+    ]
+    for copy in copies:
+        copy.start()
+    for copy in copies:
+        copy.wait()
+
+
 def per_device(queries, keys, values, level_table, level_code, out_weight, cotangent):
     rows, width = queries.shape
     vmem = pl.BlockSpec(memory_space=pltpu.VMEM)
+    hbm = pl.BlockSpec(memory_space=pltpu.MemorySpace.HBM)
     smem = pl.BlockSpec(memory_space=pltpu.SMEM)
     dma = pltpu.SemaphoreType.DMA
 
@@ -486,7 +511,7 @@
         return pltpu.VMEM(shape, F32)
 
     scratch = [
-        bf(4, rows, 512), f32(4, 6, rows, 128), f32(4, rows, rows), f32(4, rows, rows),
+        bf(rows, 512), bf(rows, 512), bf(rows, 512), bf(512, 2048), dma((5,)), bf(4, rows, 512), f32(4, 6, rows, 128), f32(4, rows, rows), f32(4, rows, rows),
         bf(4, rows, rows), bf(4, rows, 768), bf(rows, 512), bf(rows, 512),
         f32(rows, 512), f32(rows, 512), f32(rows, 512), f32(rows, 512),
         bf(512, 128), bf(512, 128), bf(256, 128), bf(NZ, 32, 128), bf(32, 128), bf(NX, 32, 128),
@@ -504,7 +529,7 @@
         dma((NZ,)), dma((NZ,)), dma((NZ,)), dma((NZ,)), dma((NX,)), dma((NX,)),
     ]
     shape = jax.ShapeDtypeStruct
-    return pl.pallas_call(
+    results = pl.pallas_call(
         kernel,
         out_shape=(
             shape((rows, width), BF16),
@@ -512,16 +537,26 @@
             shape((rows, width), BF16),
             shape((rows, width), BF16),
             shape((rows, width), BF16),
-            shape((CODES, 4), F32),
+            shape((4, CODES), F32),
         ),
-        in_specs=[vmem, vmem, vmem, smem, vmem, vmem, vmem],
+        in_specs=[hbm, hbm, hbm, smem, vmem, hbm, hbm],
         out_specs=[vmem] * 6,
         scratch_shapes=scratch,
         compiler_params=pltpu.CompilerParams(
-            collective_id=0, has_side_effects=True, vmem_limit_bytes=56 * 2**20
+            collective_id=0, has_side_effects=True, vmem_limit_bytes=53900 * 2**10
         ),
         name="layer",
-    )(queries, keys, values, level_table, level_code, out_weight, cotangent)
+    )(queries, keys, values, level_table.T, level_code.T, out_weight, cotangent)
+    stored = pl.pallas_call(
+        store,
+        out_shape=tuple(shape(value.shape, value.dtype) for value in results),
+        in_specs=[vmem] * 6,
+        out_specs=[pl.BlockSpec(memory_space=pl.ANY)] * 6,
+        scratch_shapes=[dma((6,))],
+        compiler_params=pltpu.CompilerParams(vmem_limit_bytes=2**20),
+        name="store",
+    )(*results)
+    return (*stored[:5], stored[5].T)
 
 
 def solution(mesh):

time: 71 us -> 59.1 us (0.83)
  local copies, waits for them, and re-layouts: 12.3 us -> 1.39 us
  Pallas kernels: 57.6 us -> 56.8 us
    unnamed x7 -> x4, local copies, waits for them, and re-layouts: 11 us -> 1.39 us
    pallas_call x1, Pallas kernels: 57.6 us -> 55.8 us  [per_device(): pl.pallas_call(kernel, out_shape=(shape((rows, width), BF16), shape((32,...]
    pallas_call x1 -> x0, local copies, waits for them, and re-layouts: 1.35 us -> none  [per_device(): pl.pallas_call(kernel, out_shape=(shape((rows, width), BF16), shape((32,...]
    pallas_call x0 -> x1, Pallas kernels: none -> 1.04 us  [per_device(): pl.pallas_call(store, out_shape=tuple((shape(value.shape, value.dtype) fo...]
where the time goes in v2:
time: 59.1 us; the launch traced here: 58.9 us
  Pallas kernels  56.8 us (96%)
  local copies, waits for them, and re-layouts  1.39 us (2%)
  between operations  0.65 us (1%)
    pallas_call x1, Pallas kernels, per_device(): pl.pallas_call(kernel, out_shape=(shape((rows, width), BF16), shape((32,...  55.8 us
    unnamed x4, local copies, waits for them, and re-layouts  1.39 us

profile of v2, /device:TPU:1, one launch (start us, length us, event | category | flops | bytes accessed | tf_op | source)
XLA Modules:
  0.0 58.9 jit_solution(16319244357699984567)
XLA Ops:
  0.6 0.0 copy-start
  0.6 0.7 %copy-done = s32[256,9]{0,1:T(8,128)S(1)} copy-done((s32[256,9]{0,1:T(8,128)S(1)}, s32[256,9]{0,1:T(8,128)}, u32[]{:S(2)}) %copy-start) | copy-done | bytes 9240
  1.4 0.0 copy-start.1
  1.4 0.7 %copy-done.1 = f32[16,4]{0,1:T(4,128)S(1)} copy-done((f32[16,4]{0,1:T(4,128)S(1)}, f32[16,4]{0,1:T(4,128)}, u32[]{:S(2)}) %copy-start.1) | copy-done | bytes 280
  2.0 55.8 %layer.1 = (bf16[256,512]{1,0:T(8,128)(2,1)S(1)}, f32[32,512]{1,0:T(8,128)S(1)}, bf16[256,512]{1,0:T(8,128)(2,1)S(1)}, bf16[256,512]{1,0:T(8,128)(2,1)S(1)}, bf1...) custom-call(bf16[256,512]{1,0:T(8,128)(2,1)} %q_hbm.1, bf16[256,512]{1,0:T(8,128)(2,1)} %k_hbm.1, bf16[256,512]{1,0:T(8,128)(2,1)} %v_hbm.1, ...), custom_call_target="tpu_custom_call" | custom-call | tf_op jit(solution)/shard_map/layer/pallas_call | solution.py:532
  57.8 1.0 %store.1 = (bf16[256,512]{1,0:T(8,128)(2,1)}, f32[32,512]{1,0:T(8,128)}, bf16[256,512]{1,0:T(8,128)(2,1)}, bf16[256,512]{1,0:T(8,128)(2,1)}, bf16[256,512]{1,0:T(8,128)(2,1)}, /*index=5*/f32[4,16]{1,0:T(4,128)}) custom-call(bf16[256,512]{1,0:T(8,128)(2,1)S(1)} %get-tuple-element.18.refs_0_, f32[32,512]{1,0:T(8,128)S(1)} %get-tuple-element.19.refs_1_, ...), custom_call_target="tpu_custom_call" | custom-call | tf_op jit(solution)/shard_map/store/pallas_call | solution.py:550
Async XLA Ops:
  0.6 0.7 %copy-start = (s32[256,9]{0,1:T(8,128)S(1)}, s32[256,9]{0,1:T(8,128)}, u32[]{:S(2)}) copy-start(s32[256,9]{0,1:T(8,128)} %param.11) | copy-start | bytes 27652
  1.4 0.7 %copy-start.1 = (f32[16,4]{0,1:T(4,128)S(1)}, f32[16,4]{0,1:T(4,128)}, u32[]{:S(2)}) copy-start(f32[16,4]{0,1:T(4,128)} %param.10) | copy-start | bytes 772

commit v3 on v2

--- a/solution.py
+++ b/solution.py
@@ -43,7 +43,7 @@
 def kernel(
     q_hbm, k_hbm, v_hbm, table_ref, code_ref, w_hbm, cot_hbm,
     mixed_ref, wg_ref, qg_ref, kg_ref, vg_ref, tg_ref,
-    q_ref, k_ref, v_ref, w_ref, load_sems, cotall, coefb, scores, lw, probs, sgbuf, gbuf, abuf, attnl, qgl, kgl, vgl,
+    q_ref, k_ref, v_ref, w_ref, load_sems, far_sems, reads, cotall, coefb, scores, lw, probs, sgbuf, gbuf, abuf, attnl, qgl, kgl, vgl,
     dsend, drecv, zsend_f, zrecv_f, xsend_f, xrecv_f, rsend_f, rx_f, fall,
     t0send, t0recv, tsend, trecv, zsend_b, zrecv_b, xsend_b, xrecv_b, gsend, gall,
     mpart, mrelay, mrecv, wpart, wrecv, wrelay, wxrecv, wz, wzrecv,
@@ -100,13 +100,24 @@
     def col(h):
         return slice(h * size, (h + 1) * size)
 
+    right, left = mod(y + 1, 4), mod(y - 1, 4)
+    x_right, x_left, x_opposite = mod(x + 1, 4), mod(x - 1, 4), mod(x + 2, 4)
+    z_next, z_last = mod(z + 1, NZ), mod(z - 1, NZ)
     barrier = pltpu.get_barrier_semaphore()
-    partners = [partner]
-    partners += [at_y(mod(y + off, 4)) for off in range(1, 4)]
-    partners += [at_z(mod(z + off, NZ)) for off in range(1, NZ)]
-    partners += [at_x(mod(x + off, NX)) for off in range(1, NX)]
-    for device in partners:
+    near = [partner, at_y(right), at_y(left), at_z(z_next), at_z(z_last), at_x(x_right), at_x(x_left)]
+    for device in near:
         pl.semaphore_signal(barrier, inc=1, device_id=device, device_id_type=MESH)
+
+    def tell(index, device):
+        pl.semaphore_signal(far_sems.at[index], inc=1, device_id=device, device_id_type=MESH)
+
+    def tell_z():
+        tell(0, at_z(z_next))
+        tell(1, at_z(z_last))
+
+    def hear_z():
+        pl.semaphore_wait(far_sems.at[0], 1)
+        pl.semaphore_wait(far_sems.at[1], 1)
 
     loads[1].wait()
     loads[2].wait()
@@ -117,15 +128,17 @@
         def _(l=l):
             fall[l, c] = jnp.zeros((256, size), BF16)
     loads[0].wait()
-    pl.semaphore_wait(barrier, len(partners))
-
-    right, left = mod(y + 1, 4), mod(y - 1, 4)
+    pl.semaphore_wait(barrier, len(near))
+
     top, low = pl.ds(0, half), pl.ds(half, half)
     go(remote(cotall.at[y, top], cotall.at[y, top], cot_s.at[0], cot_r.at[0], at_y(right)))
     go(remote(cotall.at[y, low], cotall.at[y, low], cot_s.at[2], cot_r.at[2], at_y(left)))
     go(remote(cotall.at[y, low], cotall.at[y, low], cot_s.at[1], cot_r.at[1], at_y(right)))
     go(remote(cotall.at[y, top], cotall.at[y, top], cot_s.at[3], cot_r.at[3], at_y(left)))
     go(remote(dsend, drecv, core_s.at[0], core_r.at[0], partner))
+    tell(2, at_x(x_right))
+    tell(3, at_x(x_left))
+    tell_z()
 
     levels = code_ref.shape[0]
     code_t = code_ref[...].astype(F32)
@@ -140,12 +153,43 @@
     for h in range(heads):
         lam = jnp.zeros((rows, size), F32)
         for entry in range(CODES):
-            lam = jnp.where(code == float(entry), table_ref[h, entry], lam)
+            lam = jnp.where(code == float(entry), table_ref[h:h + 1, entry:entry + 1], lam)
         coefs.append(lam * scale)
 
+    pl.semaphore_wait(far_sems.at[2], 1)
+    pl.semaphore_wait(far_sems.at[3], 1)
+    hear_z()
+    tell_z()
+
+    loads[3].wait()
+    row = lax.broadcasted_iota(jnp.int32, (rows, rows), 0)
+    column = lax.broadcasted_iota(jnp.int32, (rows, rows), 1)
+    row_span, column_span = row // SPAN, column // SPAN
+    in_level = [
+        (row_span == column_span) & (column <= row),
+        (row_span // 2 == column_span // 2) & (column_span < row_span),
+        (row_span >= 2) & (column_span < 2),
+    ]
+
+    def local_forward(h):
+        weight = jnp.zeros((rows, rows), F32)
+        for l in range(3):
+            weight = jnp.where(in_level[l], coefs[h][:, l:l + 1], weight)
+        score = mm(q_ref[:, col(h)], k_ref[:, col(h)], NT)
+        scores[h] = score
+        lw[h] = weight
+        prob = (score * weight).astype(BF16)
+        probs[h] = prob
+        attnl[:, col(h)] = mm(prob, v_ref[:, col(h)], NN)
+
+    for h in range(2):
+        local_forward(h)
+    hear_z()
+    tell_z()
     arrived(drecv, core_r.at[0])
     half_rows = pl.ds(pl.multiple_of(c * 256, 256), 256)
     zsend_f[...] = (dsend[half_rows, :].astype(F32) + drecv[half_rows, :].astype(F32)).astype(BF16)
+    hear_z()
     for off in range(1, NZ):
         zt = mod(z + off, NZ)
         go(remote(zsend_f.at[pl.ds(pl.multiple_of(zt * 32, 32), 32)], zrecv_f.at[z],
@@ -153,6 +197,8 @@
     own_slice = pl.ds(pl.multiple_of(z * 32, 32), 32)
     zrecv_f[z] = zsend_f[own_slice, :]
 
+    for h in range(2, heads):
+        local_forward(h)
     for h in range(heads):
         for l in range(3, levels):
             coefb[h, l - 3] = jnp.broadcast_to(coefs[h][:, l:l + 1], (rows, size))
@@ -188,26 +234,6 @@
         def _(l=l):
             fall[l, c, own_slice, :] = rsend_f[z, l]
 
-    loads[3].wait()
-    row = lax.broadcasted_iota(jnp.int32, (rows, rows), 0)
-    column = lax.broadcasted_iota(jnp.int32, (rows, rows), 1)
-    row_span, column_span = row // SPAN, column // SPAN
-    in_level = [
-        (row_span == column_span) & (column <= row),
-        (row_span // 2 == column_span // 2) & (column_span < row_span),
-        (row_span >= 2) & (column_span < 2),
-    ]
-    for h in range(heads):
-        weight = jnp.zeros((rows, rows), F32)
-        for l in range(3):
-            weight = jnp.where(in_level[l], coefs[h][:, l:l + 1], weight)
-        score = mm(q_ref[:, col(h)], k_ref[:, col(h)], NT)
-        scores[h] = score
-        lw[h] = weight
-        prob = (score * weight).astype(BF16)
-        probs[h] = prob
-        attnl[:, col(h)] = mm(prob, v_ref[:, col(h)], NN)
-
     for off in range(1, NX):
         xs = mod(x - off, NX)
         arrived(xrecv_f.at[xs], xf_r.at[off], xs < x)
@@ -249,6 +275,75 @@
     go(remote(tsend.at[:, other], trecv, core_s.at[1], core_r.at[1], partner))
     go(remote(t0send, t0recv, core_s.at[2], core_r.at[2], partner))
 
+    for off in range(1, NZ):
+        zs = mod(z - off, NZ)
+        zs_slice = pl.ds(pl.multiple_of(zs * 32, 32), 32)
+        for l in range(5):
+            arrived(fall.at[l, c, zs_slice], rf_r.at[off, l], level_bits[l] == 1)
+    go(remote(fall.at[:, c], fall.at[:, c], core_s.at[3], core_r.at[3], partner))
+
+    arrived(trecv, core_r.at[1])
+    for l in range(5):
+        zsend_b[l] = (tsend[l, c].astype(F32) + trecv[l].astype(F32)).astype(BF16)
+    for off in range(1, NZ):
+        zt = mod(z + off, NZ)
+        for l in range(5):
+            go(remote(zsend_b.at[l, pl.ds(pl.multiple_of(zt * 32, 32), 32)], zrecv_b.at[z, l],
+                      zb_s.at[off, l], zb_r.at[off, l], at_z(zt)), level_bits[l] == 1)
+    for l in range(5):
+        @pl.when(level_bits[l] == 1)
+        def _(l=l):
+            zrecv_b[z, l] = zsend_b[l, own_slice, :]
+
+    arrived(fall.at[:, other], core_r.at[3])
+
+    def found_states(h):
+        found = [jnp.where(c == 1, drecv[col(h), :], jnp.zeros((size, size), BF16))]
+        found += [fall[l, h // 2, col(h % 2), :] for l in range(5)]
+        return jnp.concatenate(found, axis=1)
+
+    for h in range(heads):
+        values = mm(q_ref[:, col(h)], found_states(h), NN)
+        reads[h] = values
+        attention = attnl[:, col(h)]
+        for l in range(6):
+            attention = attention + coefb[h, l] * values[:, col(l)]
+        abuf[:, col(h)] = attention.astype(BF16)
+
+    def weight_part(step, target):
+        part = mm(cotall[target], abuf[...], TN)
+        for block in range(16):
+            wpart[target, block % 2, pl.ds((block // 2) * 32, 32), :] = (
+                part[block * 32:(block + 1) * 32].astype(BF16)
+            )
+        go(remote(wpart.at[target, other], wrecv.at[target], wc_s.at[step], wc_r.at[step], partner))
+
+    def weight_chip(step, target):
+        arrived(wrecv.at[target], wc_r.at[step])
+        wpart[target, c] = (wpart[target, c].astype(F32) + wrecv[target].astype(F32)).astype(BF16)
+
+    def product_for(target):
+        columns = pl.ds(pl.multiple_of(target * 512, 512), 512)
+        mpart[target] = mm(abuf[...], w_ref[:, columns], NN).astype(BF16)
+
+    sides = [pl.ds(0, 256), pl.ds(256, 256)]
+    weight_part(0, x_opposite)
+    product_for(opposite)
+    go(remote(mpart.at[opposite, top], mrelay.at[0], m_s.at[0], m_r.at[0], at_y(left)))
+    go(remote(mpart.at[opposite, low], mrelay.at[1], m_s.at[1], m_r.at[1], at_y(right)))
+    weight_part(1, x_left)
+    weight_chip(0, x_opposite)
+    for i in range(2):
+        go(remote(wpart.at[x_opposite, c, top, sides[i]], wrelay.at[0, :, sides[i]],
+                  wx_s.at[4 * i], wx_r.at[4 * i], at_x(x_left)))
+        go(remote(wpart.at[x_opposite, c, low, sides[i]], wrelay.at[1, :, sides[i]],
+                  wx_s.at[4 * i + 1], wx_r.at[4 * i + 1], at_x(x_right)))
+    weight_part(2, x_right)
+    product_for(left)
+    product_for(right)
+    weight_chip(1, x_left)
+    weight_chip(2, x_right)
+
     entry_row = lax.broadcasted_iota(jnp.int32, (CODES, rows), 0).astype(F32)
     one_hot = [
         jnp.where(jnp.broadcast_to(code_t[l:l + 1, :], (CODES, rows)) == entry_row, 1.0, 0.0).astype(BF16)
@@ -265,104 +360,13 @@
         for l in range(3):
             masked = jnp.where(in_level[l], product, 0.0).astype(BF16)
             total = total + scales[l] * mm(one_hot[l], masked, NN)
-        table_parts.append(total[:, :size] + total[:, size:])
         qgl[:, col(h)] = mm(score_grad, k_ref[:, col(h)], NN)
         kgl[:, col(h)] = mm(score_grad, q_ref[:, col(h)], TN)
         vgl[:, col(h)] = mm(probs[h], grad, TN)
-
-    for h in range(2):
+        table_parts.append(total[:, :size] + total[:, size:])
+
+    for h in range(heads):
         local_back(h)
-
-    arrived(trecv, core_r.at[1])
-    for l in range(5):
-        zsend_b[l] = (tsend[l, c].astype(F32) + trecv[l].astype(F32)).astype(BF16)
-    for off in range(1, NZ):
-        zt = mod(z + off, NZ)
-        for l in range(5):
-            go(remote(zsend_b.at[l, pl.ds(pl.multiple_of(zt * 32, 32), 32)], zrecv_b.at[z, l],
-                      zb_s.at[off, l], zb_r.at[off, l], at_z(zt)), level_bits[l] == 1)
-    for l in range(5):
-        @pl.when(level_bits[l] == 1)
-        def _(l=l):
-            zrecv_b[z, l] = zsend_b[l, own_slice, :]
-
-    for off in range(1, NZ):
-        zs = mod(z - off, NZ)
-        zs_slice = pl.ds(pl.multiple_of(zs * 32, 32), 32)
-        for l in range(5):
-            arrived(fall.at[l, c, zs_slice], rf_r.at[off, l], level_bits[l] == 1)
-    go(remote(fall.at[:, c], fall.at[:, c], core_s.at[3], core_r.at[3], partner))
-
-    for h in range(2, heads):
-        local_back(h)
-
-    arrived(fall.at[:, other], core_r.at[3])
-
-    for h in range(heads):
-        query, grad = q_ref[:, col(h)], gbuf[:, col(h)].astype(F32)
-        found = [jnp.where(c == 1, drecv[col(h), :], jnp.zeros((size, size), BF16))]
-        found += [fall[l, h // 2, col(h % 2), :] for l in range(5)]
-        found = jnp.concatenate(found, axis=1)
-        reads = mm(query, found, NN)
-        attention = attnl[:, col(h)]
-        total = table_parts[h]
-        for l in range(6):
-            read = reads[:, col(l)]
-            attention = attention + coefb[h, l] * read
-            total = total + scales[l + 3] * mm(one_hot[l + 3], (grad * read).astype(BF16), NN)
-        table_parts[h] = total
-        abuf[:, col(h)] = attention.astype(BF16)
-        qg_ref[:, col(h)] = (qgl[:, col(h)] + mm(sgbuf[h], found, NT)).astype(BF16)
-
-    def product_for(target):
-        columns = pl.ds(pl.multiple_of(target * 512, 512), 512)
-        mpart[target] = mm(abuf[...], w_ref[:, columns], NN).astype(BF16)
-
-    product_for(opposite)
-    go(remote(mpart.at[opposite, top], mrelay.at[0], m_s.at[0], m_r.at[0], at_y(left)))
-    go(remote(mpart.at[opposite, low], mrelay.at[1], m_s.at[1], m_r.at[1], at_y(right)))
-
-    x_right, x_left, x_opposite = mod(x + 1, 4), mod(x - 1, 4), mod(x + 2, 4)
-
-    def weight_part(step, target):
-        part = mm(cotall[target], abuf[...], TN)
-        for block in range(16):
-            wpart[target, block % 2, pl.ds((block // 2) * 32, 32), :] = (
-                part[block * 32:(block + 1) * 32].astype(BF16)
-            )
-        go(remote(wpart.at[target, other], wrecv.at[target], wc_s.at[step], wc_r.at[step], partner))
-
-    weight_part(0, x_opposite)
-    product_for(left)
-    product_for(right)
-    weight_part(1, x_left)
-
-    def weight_chip(step, target):
-        arrived(wrecv.at[target], wc_r.at[step])
-        wpart[target, c] = (wpart[target, c].astype(F32) + wrecv[target].astype(F32)).astype(BF16)
-
-    weight_chip(0, x_opposite)
-    go(remote(wpart.at[x_opposite, c, top], wrelay.at[0], wx_s.at[0], wx_r.at[0], at_x(x_left)))
-    go(remote(wpart.at[x_opposite, c, low], wrelay.at[1], wx_s.at[1], wx_r.at[1], at_x(x_right)))
-
-    arrived(mrelay.at[0], m_r.at[0])
-    mpart[left, top] = (mpart[left, top].astype(F32) + mrelay[0].astype(F32)).astype(BF16)
-    go(remote(mpart.at[left], mrecv.at[0], m_s.at[2], m_r.at[2], at_y(left)))
-    arrived(mrelay.at[1], m_r.at[1])
-    mpart[right, low] = (mpart[right, low].astype(F32) + mrelay[1].astype(F32)).astype(BF16)
-    go(remote(mpart.at[right], mrecv.at[1], m_s.at[3], m_r.at[3], at_y(right)))
-
-    weight_part(2, x_right)
-    weight_part(3, x)
-    product_for(y)
-
-    lane128 = lax.broadcasted_iota(jnp.int32, (CODES, size), 1)
-    partial_table = jnp.zeros((CODES, size), F32)
-    for h in range(heads):
-        summed = jnp.sum(table_parts[h], axis=1, keepdims=True)
-        partial_table = jnp.where(lane128 == h, summed, partial_table)
-    tgsend[...] = partial_table
-    go(remote(tgsend, tgcore, core_s.at[4], core_r.at[4], partner))
 
     for off in range(1, NZ):
         zs = mod(z - off, NZ)
@@ -381,20 +385,25 @@
         bit = jnp.where(lax.div(x, 2) == lax.div(xt, 2), 0, 1)
         go(remote(xsend_b.at[bit], xrecv_b.at[x], xb_s.at[off], xb_r.at[off], at_x(xt)), xt < x)
 
-    weight_chip(1, x_left)
-    weight_chip(2, x_right)
-    arrived(wrelay.at[0], wx_r.at[0])
-    wpart[x_left, c, top] = (wpart[x_left, c, top].astype(F32) + wrelay[0].astype(F32)).astype(BF16)
-    go(remote(wpart.at[x_left, c], wxrecv.at[0], wx_s.at[2], wx_r.at[2], at_x(x_left)))
-    arrived(wrelay.at[1], wx_r.at[1])
-    wpart[x_right, c, low] = (wpart[x_right, c, low].astype(F32) + wrelay[1].astype(F32)).astype(BF16)
-    go(remote(wpart.at[x_right, c], wxrecv.at[1], wx_s.at[3], wx_r.at[3], at_x(x_right)))
-
-    arrived(tgcore, core_r.at[4])
-    tgzsend[...] = tgsend[...] + tgcore[...]
-    for off in range(1, NZ):
-        go(remote(tgzsend, tgz.at[z], tz_s.at[off], tz_r.at[off], at_z(mod(z + off, NZ))))
-    tgz[z] = tgzsend[...]
+    def weight_relay(i):
+        side = sides[i]
+        arrived(wrelay.at[0, :, side], wx_r.at[4 * i])
+        wpart[x_left, c, top, side] = (
+            wpart[x_left, c, top, side].astype(F32) + wrelay[0, :, side].astype(F32)
+        ).astype(BF16)
+        go(remote(wpart.at[x_left, c, :, side], wxrecv.at[0, :, side],
+                  wx_s.at[4 * i + 2], wx_r.at[4 * i + 2], at_x(x_left)))
+        arrived(wrelay.at[1, :, side], wx_r.at[4 * i + 1])
+        wpart[x_right, c, low, side] = (
+            wpart[x_right, c, low, side].astype(F32) + wrelay[1, :, side].astype(F32)
+        ).astype(BF16)
+        go(remote(wpart.at[x_right, c, :, side], wxrecv.at[1, :, side],
+                  wx_s.at[4 * i + 3], wx_r.at[4 * i + 3], at_x(x_right)))
+
+    weight_relay(0)
+    weight_part(3, x)
+    product_for(y)
+    weight_relay(1)
 
     for off in range(1, NX):
         xs = mod(x - off, NX)
@@ -420,23 +429,54 @@
         go(remote(gsend.at[zt], gall.at[c, own_slice], rb_s.at[off], rb_r.at[off], at_z(zt)))
     gall[c, own_slice, :] = gsend[z]
 
+    arrived(mrelay.at[0], m_r.at[0])
+    mpart[left, top] = (mpart[left, top].astype(F32) + mrelay[0].astype(F32)).astype(BF16)
+    go(remote(mpart.at[left], mrecv.at[0], m_s.at[2], m_r.at[2], at_y(left)))
+    arrived(mrelay.at[1], m_r.at[1])
+    mpart[right, low] = (mpart[right, low].astype(F32) + mrelay[1].astype(F32)).astype(BF16)
+    go(remote(mpart.at[right], mrecv.at[1], m_s.at[3], m_r.at[3], at_y(right)))
+
+    for h in range(heads):
+        grad = gbuf[:, col(h)].astype(F32)
+        total = table_parts[h]
+        for l in range(6):
+            total = total + scales[l + 3] * mm(one_hot[l + 3], (grad * reads[h, :, col(l)]).astype(BF16), NN)
+        table_parts[h] = total
+        qg_ref[:, col(h)] = (qgl[:, col(h)] + mm(sgbuf[h], found_states(h), NT)).astype(BF16)
+    lane128 = lax.broadcasted_iota(jnp.int32, (CODES, size), 1)
+    partial_table = jnp.zeros((CODES, size), F32)
+    for h in range(heads):
+        summed = jnp.sum(table_parts[h], axis=1, keepdims=True)
+        partial_table = jnp.where(lane128 == h, summed, partial_table)
+    tgsend[...] = partial_table
+    go(remote(tgsend, tgcore, core_s.at[4], core_r.at[4], partner))
+
+    arrived(tgcore, core_r.at[4])
+    tgzsend[...] = tgsend[...] + tgcore[...]
+    for off in range(1, NZ):
+        go(remote(tgzsend, tgz.at[z], tz_s.at[off], tz_r.at[off], at_z(mod(z + off, NZ))))
+    tgz[z] = tgzsend[...]
     weight_chip(3, x)
 
+    def weight_ring(i):
+        side = sides[i]
+        arrived(wxrecv.at[0, :, side], wx_r.at[4 * i + 2])
+        arrived(wxrecv.at[1, :, side], wx_r.at[4 * i + 3])
+        wz[:, side] = (
+            wpart[x, c, :, side].astype(F32) + wxrecv[0, :, side].astype(F32) + wxrecv[1, :, side].astype(F32)
+        ).astype(BF16)
+        for off in range(1, NZ):
+            zt = mod(z + off, NZ)
+            go(remote(wz.at[pl.ds(pl.multiple_of(zt * 32, 32), 32), side], wzrecv.at[z, :, side],
+                      wz_s.at[off, i], wz_r.at[off, i], at_z(zt)))
+        wzrecv[z, :, side] = wz[own_slice, side]
+
+    weight_ring(0)
     for off in range(1, NZ):
         zs = mod(z - off, NZ)
         arrived(gall.at[c, pl.ds(pl.multiple_of(zs * 32, 32), 32)], rb_r.at[off])
     go(remote(gall.at[c], gall.at[c], core_s.at[5], core_r.at[5], partner))
-
-    arrived(wxrecv.at[0], wx_r.at[2])
-    arrived(wxrecv.at[1], wx_r.at[3])
-    wz[...] = (
-        wpart[x, c].astype(F32) + wxrecv[0].astype(F32) + wxrecv[1].astype(F32)
-    ).astype(BF16)
-    for off in range(1, NZ):
-        zt = mod(z + off, NZ)
-        go(remote(wz.at[pl.ds(pl.multiple_of(zt * 32, 32), 32)], wzrecv.at[z],
-                  wz_s.at[off], wz_r.at[off], at_z(zt)))
-    wzrecv[z] = wz[own_slice, :]
+    weight_ring(1)
 
     for off in range(1, NZ):
         arrived(tgz.at[mod(z - off, NZ)], tz_r.at[off])
@@ -471,12 +511,13 @@
     square = jnp.concatenate([table, jnp.zeros((size - CODES, size), F32)], axis=0)
     tg_ref[...] = square.T[:heads, :CODES] * (1.0 / math.sqrt(tokens * levels))
 
-    for off in range(1, NZ):
-        arrived(wzrecv.at[mod(z - off, NZ)], wz_r.at[off])
-    weight = wzrecv[0].astype(F32)
-    for zs in range(1, NZ):
-        weight = weight + wzrecv[zs].astype(F32)
-    wg_ref[...] = weight * (1.0 / math.sqrt(tokens))
+    for i in range(2):
+        for off in range(1, NZ):
+            arrived(wzrecv.at[mod(z - off, NZ), :, sides[i]], wz_r.at[off, i])
+        weight = wzrecv[0, :, sides[i]].astype(F32)
+        for zs in range(1, NZ):
+            weight = weight + wzrecv[zs, :, sides[i]].astype(F32)
+        wg_ref[:, sides[i]] = weight * (1.0 / math.sqrt(tokens))
 
     for copy, cond in pending:
         if cond is None:
@@ -501,7 +542,6 @@
     rows, width = queries.shape
     vmem = pl.BlockSpec(memory_space=pltpu.VMEM)
     hbm = pl.BlockSpec(memory_space=pltpu.MemorySpace.HBM)
-    smem = pl.BlockSpec(memory_space=pltpu.SMEM)
     dma = pltpu.SemaphoreType.DMA
 
     def bf(*shape):
@@ -511,7 +551,8 @@
         return pltpu.VMEM(shape, F32)
 
     scratch = [
-        bf(rows, 512), bf(rows, 512), bf(rows, 512), bf(512, 2048), dma((5,)), bf(4, rows, 512), f32(4, 6, rows, 128), f32(4, rows, rows), f32(4, rows, rows),
+        bf(rows, 512), bf(rows, 512), bf(rows, 512), bf(512, 2048), dma((5,)),
+        pltpu.SemaphoreType.REGULAR((4,)), f32(4, rows, 768), bf(4, rows, 512), f32(4, 6, rows, 128), f32(4, rows, rows), f32(4, rows, rows),
         bf(4, rows, rows), bf(4, rows, 768), bf(rows, 512), bf(rows, 512),
         f32(rows, 512), f32(rows, 512), f32(rows, 512), f32(rows, 512),
         bf(512, 128), bf(512, 128), bf(256, 128), bf(NZ, 32, 128), bf(32, 128), bf(NX, 32, 128),
@@ -525,8 +566,8 @@
         f32(CODES, 128), f32(NX, CODES, 128),
         dma((6,)), dma((6,)), dma((6,)), dma((6,)), dma((NZ,)), dma((NZ,)), dma((NX,)), dma((NX,)),
         dma((NZ, 5)), dma((NZ, 5)), dma((NZ, 5)), dma((NZ, 5)), dma((NX,)), dma((NX,)),
-        dma((NZ,)), dma((NZ,)), dma((4,)), dma((4,)), dma((4,)), dma((4,)), dma((4,)), dma((4,)),
-        dma((NZ,)), dma((NZ,)), dma((NZ,)), dma((NZ,)), dma((NX,)), dma((NX,)),
+        dma((NZ,)), dma((NZ,)), dma((4,)), dma((4,)), dma((4,)), dma((4,)), dma((8,)), dma((8,)),
+        dma((NZ, 2)), dma((NZ, 2)), dma((NZ,)), dma((NZ,)), dma((NX,)), dma((NX,)),
     ]
     shape = jax.ShapeDtypeStruct
     results = pl.pallas_call(
@@ -539,7 +580,7 @@
             shape((rows, width), BF16),
             shape((4, CODES), F32),
         ),
-        in_specs=[hbm, hbm, hbm, smem, vmem, hbm, hbm],
+        in_specs=[hbm, hbm, hbm, vmem, vmem, hbm, hbm],
         out_specs=[vmem] * 6,
         scratch_shapes=scratch,
         compiler_params=pltpu.CompilerParams(

time: 59.1 us -> 55.3 us (0.936)
  Pallas kernels: 56.8 us -> 53.1 us
    pallas_call x1, Pallas kernels: 55.8 us -> 52 us  [per_device(): pl.pallas_call(kernel, out_shape=(shape((rows, width), BF16), shape((32,...]
where the time goes in v3:
time: 55.3 us; the launch traced here: 55.1 us
  Pallas kernels  53.1 us (96%)
  local copies, waits for them, and re-layouts  1.39 us (3%)
  between operations  0.65 us (1%)
    pallas_call x1, Pallas kernels, per_device(): pl.pallas_call(kernel, out_shape=(shape((rows, width), BF16), shape((32,...  52 us
    unnamed x4, local copies, waits for them, and re-layouts  1.39 us

profile of v3, /device:TPU:1, one launch (start us, length us, event | category | flops | bytes accessed | tf_op | source)
XLA Modules:
  0.0 55.1 jit_solution(12606620434083616859)
XLA Ops:
  0.6 0.0 copy-start
  0.6 0.7 %copy-done = s32[256,9]{0,1:T(8,128)S(1)} copy-done((s32[256,9]{0,1:T(8,128)S(1)}, s32[256,9]{0,1:T(8,128)}, u32[]{:S(2)}) %copy-start) | copy-done | bytes 9240
  1.4 0.0 copy-start.1
  1.4 0.7 %copy-done.1 = f32[16,4]{0,1:T(4,128)S(1)} copy-done((f32[16,4]{0,1:T(4,128)S(1)}, f32[16,4]{0,1:T(4,128)}, u32[]{:S(2)}) %copy-start.1) | copy-done | bytes 280
  2.0 52.0 %layer.1 = (bf16[256,512]{1,0:T(8,128)(2,1)S(1)}, f32[32,512]{1,0:T(8,128)S(1)}, bf16[256,512]{1,0:T(8,128)(2,1)S(1)}, bf16[256,512]{1,0:T(8,128)(2,1)S(1)}, bf1...) custom-call(bf16[256,512]{1,0:T(8,128)(2,1)} %q_hbm.1, bf16[256,512]{1,0:T(8,128)(2,1)} %k_hbm.1, bf16[256,512]{1,0:T(8,128)(2,1)} %v_hbm.1, ...), custom_call_target="tpu_custom_call" | custom-call | tf_op jit(solution)/shard_map/layer/pallas_call | solution.py:573
  54.1 1.0 %store.1 = (bf16[256,512]{1,0:T(8,128)(2,1)}, f32[32,512]{1,0:T(8,128)}, bf16[256,512]{1,0:T(8,128)(2,1)}, bf16[256,512]{1,0:T(8,128)(2,1)}, bf16[256,512]{1,0:T(8,128)(2,1)}, /*index=5*/f32[4,16]{1,0:T(4,128)}) custom-call(bf16[256,512]{1,0:T(8,128)(2,1)S(1)} %get-tuple-element.18.refs_0_, f32[32,512]{1,0:T(8,128)S(1)} %get-tuple-element.19.refs_1_, ...), custom_call_target="tpu_custom_call" | custom-call | tf_op jit(solution)/shard_map/store/pallas_call | solution.py:591
Async XLA Ops:
  0.6 0.7 %copy-start = (s32[256,9]{0,1:T(8,128)S(1)}, s32[256,9]{0,1:T(8,128)}, u32[]{:S(2)}) copy-start(s32[256,9]{0,1:T(8,128)} %param.11) | copy-start | bytes 27652
  1.4 0.7 %copy-start.1 = (f32[16,4]{0,1:T(4,128)S(1)}, f32[16,4]{0,1:T(4,128)}, u32[]{:S(2)}) copy-start(f32[16,4]{0,1:T(4,128)} %param.10) | copy-start | bytes 772

commit v4 on v3

--- a/solution.py
+++ b/solution.py
@@ -10,6 +10,8 @@
 SPAN = 64
 CODES = 16
 NX, NZ = 4, 8
+Z_ORDER = (4, 3, 5, 2, 6, 1, 7)
+PIECES = 4
 F32, BF16 = jnp.float32, jnp.bfloat16
 MESH = pl.DeviceIdType.MESH
 NN = (((1,), (0,)), ((), ()))
@@ -102,9 +104,9 @@
 
     right, left = mod(y + 1, 4), mod(y - 1, 4)
     x_right, x_left, x_opposite = mod(x + 1, 4), mod(x - 1, 4), mod(x + 2, 4)
-    z_next, z_last = mod(z + 1, NZ), mod(z - 1, NZ)
     barrier = pltpu.get_barrier_semaphore()
-    near = [partner, at_y(right), at_y(left), at_z(z_next), at_z(z_last), at_x(x_right), at_x(x_left)]
+    near = [partner, at_y(right), at_y(left), at_x(x_right), at_x(x_left), at_x(x_opposite)]
+    near += [at_z(mod(z + off, NZ)) for off in (1, -1, 2, -2)]
     for device in near:
         pl.semaphore_signal(barrier, inc=1, device_id=device, device_id_type=MESH)
 
@@ -112,8 +114,8 @@
         pl.semaphore_signal(far_sems.at[index], inc=1, device_id=device, device_id_type=MESH)
 
     def tell_z():
-        tell(0, at_z(z_next))
-        tell(1, at_z(z_last))
+        tell(0, at_z(mod(z + 2, NZ)))
+        tell(1, at_z(mod(z - 2, NZ)))
 
     def hear_z():
         pl.semaphore_wait(far_sems.at[0], 1)
@@ -136,8 +138,6 @@
     go(remote(cotall.at[y, low], cotall.at[y, low], cot_s.at[1], cot_r.at[1], at_y(right)))
     go(remote(cotall.at[y, top], cotall.at[y, top], cot_s.at[3], cot_r.at[3], at_y(left)))
     go(remote(dsend, drecv, core_s.at[0], core_r.at[0], partner))
-    tell(2, at_x(x_right))
-    tell(3, at_x(x_left))
     tell_z()
 
     levels = code_ref.shape[0]
@@ -156,11 +156,6 @@
             lam = jnp.where(code == float(entry), table_ref[h:h + 1, entry:entry + 1], lam)
         coefs.append(lam * scale)
 
-    pl.semaphore_wait(far_sems.at[2], 1)
-    pl.semaphore_wait(far_sems.at[3], 1)
-    hear_z()
-    tell_z()
-
     loads[3].wait()
     row = lax.broadcasted_iota(jnp.int32, (rows, rows), 0)
     column = lax.broadcasted_iota(jnp.int32, (rows, rows), 1)
@@ -184,13 +179,11 @@
 
     for h in range(2):
         local_forward(h)
-    hear_z()
-    tell_z()
     arrived(drecv, core_r.at[0])
     half_rows = pl.ds(pl.multiple_of(c * 256, 256), 256)
     zsend_f[...] = (dsend[half_rows, :].astype(F32) + drecv[half_rows, :].astype(F32)).astype(BF16)
     hear_z()
-    for off in range(1, NZ):
+    for off in Z_ORDER:
         zt = mod(z + off, NZ)
         go(remote(zsend_f.at[pl.ds(pl.multiple_of(zt * 32, 32), 32)], zrecv_f.at[z],
                   zf_s.at[off], zf_r.at[off], at_z(zt)))
@@ -224,7 +217,7 @@
             rsend_f[zt, 1] = pairs[2 * (zt // 4)].astype(BF16)
         if zt & 4:
             rsend_f[zt, 2] = quads[0].astype(BF16)
-    for off in range(1, NZ):
+    for off in Z_ORDER:
         zt = mod(z + off, NZ)
         for l in range(3):
             go(remote(rsend_f.at[zt, l], fall.at[l, c, own_slice],
@@ -249,7 +242,7 @@
         rx_f[1] = both
         fall[4, c, own_slice, :] = both
 
-    for off in range(1, NZ):
+    for off in Z_ORDER:
         zt = mod(z + off, NZ)
         for l in range(3, 5):
             go(remote(rx_f.at[l - 3], fall.at[l, c, own_slice],
@@ -285,7 +278,7 @@
     arrived(trecv, core_r.at[1])
     for l in range(5):
         zsend_b[l] = (tsend[l, c].astype(F32) + trecv[l].astype(F32)).astype(BF16)
-    for off in range(1, NZ):
+    for off in Z_ORDER:
         zt = mod(z + off, NZ)
         for l in range(5):
             go(remote(zsend_b.at[l, pl.ds(pl.multiple_of(zt * 32, 32), 32)], zrecv_b.at[z, l],
@@ -326,14 +319,14 @@
         columns = pl.ds(pl.multiple_of(target * 512, 512), 512)
         mpart[target] = mm(abuf[...], w_ref[:, columns], NN).astype(BF16)
 
-    sides = [pl.ds(0, 256), pl.ds(256, 256)]
+    sides = [pl.ds(128 * i, 128) for i in range(PIECES)]
     weight_part(0, x_opposite)
     product_for(opposite)
     go(remote(mpart.at[opposite, top], mrelay.at[0], m_s.at[0], m_r.at[0], at_y(left)))
     go(remote(mpart.at[opposite, low], mrelay.at[1], m_s.at[1], m_r.at[1], at_y(right)))
     weight_part(1, x_left)
     weight_chip(0, x_opposite)
-    for i in range(2):
+    for i in range(PIECES):
         go(remote(wpart.at[x_opposite, c, top, sides[i]], wrelay.at[0, :, sides[i]],
                   wx_s.at[4 * i], wx_r.at[4 * i], at_x(x_left)))
         go(remote(wpart.at[x_opposite, c, low, sides[i]], wrelay.at[1, :, sides[i]],
@@ -341,9 +334,6 @@
     weight_part(2, x_right)
     product_for(left)
     product_for(right)
-    weight_chip(1, x_left)
-    weight_chip(2, x_right)
-
     entry_row = lax.broadcasted_iota(jnp.int32, (CODES, rows), 0).astype(F32)
     one_hot = [
         jnp.where(jnp.broadcast_to(code_t[l:l + 1, :], (CODES, rows)) == entry_row, 1.0, 0.0).astype(BF16)
@@ -365,9 +355,28 @@
         vgl[:, col(h)] = mm(probs[h], grad, TN)
         table_parts.append(total[:, :size] + total[:, size:])
 
-    for h in range(heads):
+    for h in range(3):
         local_back(h)
 
+    weight_chip(1, x_left)
+    weight_chip(2, x_right)
+
+    def weight_relay(i):
+        side = sides[i]
+        arrived(wrelay.at[0, :, side], wx_r.at[4 * i])
+        wpart[x_left, c, top, side] = (
+            wpart[x_left, c, top, side].astype(F32) + wrelay[0, :, side].astype(F32)
+        ).astype(BF16)
+        go(remote(wpart.at[x_left, c, :, side], wxrecv.at[0, :, side],
+                  wx_s.at[4 * i + 2], wx_r.at[4 * i + 2], at_x(x_left)))
+        arrived(wrelay.at[1, :, side], wx_r.at[4 * i + 1])
+        wpart[x_right, c, low, side] = (
+            wpart[x_right, c, low, side].astype(F32) + wrelay[1, :, side].astype(F32)
+        ).astype(BF16)
+        go(remote(wpart.at[x_right, c, :, side], wxrecv.at[1, :, side],
+                  wx_s.at[4 * i + 3], wx_r.at[4 * i + 3], at_x(x_right)))
+
+    weight_relay(0)
     for off in range(1, NZ):
         zs = mod(z - off, NZ)
         for l in range(5):
@@ -385,25 +394,12 @@
         bit = jnp.where(lax.div(x, 2) == lax.div(xt, 2), 0, 1)
         go(remote(xsend_b.at[bit], xrecv_b.at[x], xb_s.at[off], xb_r.at[off], at_x(xt)), xt < x)
 
-    def weight_relay(i):
-        side = sides[i]
-        arrived(wrelay.at[0, :, side], wx_r.at[4 * i])
-        wpart[x_left, c, top, side] = (
-            wpart[x_left, c, top, side].astype(F32) + wrelay[0, :, side].astype(F32)
-        ).astype(BF16)
-        go(remote(wpart.at[x_left, c, :, side], wxrecv.at[0, :, side],
-                  wx_s.at[4 * i + 2], wx_r.at[4 * i + 2], at_x(x_left)))
-        arrived(wrelay.at[1, :, side], wx_r.at[4 * i + 1])
-        wpart[x_right, c, low, side] = (
-            wpart[x_right, c, low, side].astype(F32) + wrelay[1, :, side].astype(F32)
-        ).astype(BF16)
-        go(remote(wpart.at[x_right, c, :, side], wxrecv.at[1, :, side],
-                  wx_s.at[4 * i + 3], wx_r.at[4 * i + 3], at_x(x_right)))
-
-    weight_relay(0)
+    local_back(3)
+    weight_relay(1)
     weight_part(3, x)
     product_for(y)
-    weight_relay(1)
+    for i in range(2, PIECES):
+        weight_relay(i)
 
     for off in range(1, NX):
         xs = mod(x - off, NX)
@@ -424,11 +420,26 @@
         if zt & 4 == 0:
             total = total + quad
         gsend[zt] = total.astype(BF16)
-    for off in range(1, NZ):
+    for off in Z_ORDER:
         zt = mod(z + off, NZ)
         go(remote(gsend.at[zt], gall.at[c, own_slice], rb_s.at[off], rb_r.at[off], at_z(zt)))
     gall[c, own_slice, :] = gsend[z]
 
+    def weight_ring(i):
+        side = sides[i]
+        arrived(wxrecv.at[0, :, side], wx_r.at[4 * i + 2])
+        arrived(wxrecv.at[1, :, side], wx_r.at[4 * i + 3])
+        wz[:, side] = (
+            wpart[x, c, :, side].astype(F32) + wxrecv[0, :, side].astype(F32) + wxrecv[1, :, side].astype(F32)
+        ).astype(BF16)
+        for off in Z_ORDER:
+            zt = mod(z + off, NZ)
+            go(remote(wz.at[pl.ds(pl.multiple_of(zt * 32, 32), 32), side], wzrecv.at[z, :, side],
+                      wz_s.at[off, i], wz_r.at[off, i], at_z(zt)))
+        wzrecv[z, :, side] = wz[own_slice, side]
+
+    weight_chip(3, x)
+    weight_ring(0)
     arrived(mrelay.at[0], m_r.at[0])
     mpart[left, top] = (mpart[left, top].astype(F32) + mrelay[0].astype(F32)).astype(BF16)
     go(remote(mpart.at[left], mrecv.at[0], m_s.at[2], m_r.at[2], at_y(left)))
@@ -451,33 +462,20 @@
     tgsend[...] = partial_table
     go(remote(tgsend, tgcore, core_s.at[4], core_r.at[4], partner))
 
+    weight_ring(1)
     arrived(tgcore, core_r.at[4])
     tgzsend[...] = tgsend[...] + tgcore[...]
     for off in range(1, NZ):
         go(remote(tgzsend, tgz.at[z], tz_s.at[off], tz_r.at[off], at_z(mod(z + off, NZ))))
     tgz[z] = tgzsend[...]
-    weight_chip(3, x)
-
-    def weight_ring(i):
-        side = sides[i]
-        arrived(wxrecv.at[0, :, side], wx_r.at[4 * i + 2])
-        arrived(wxrecv.at[1, :, side], wx_r.at[4 * i + 3])
-        wz[:, side] = (
-            wpart[x, c, :, side].astype(F32) + wxrecv[0, :, side].astype(F32) + wxrecv[1, :, side].astype(F32)
-        ).astype(BF16)
-        for off in range(1, NZ):
-            zt = mod(z + off, NZ)
-            go(remote(wz.at[pl.ds(pl.multiple_of(zt * 32, 32), 32), side], wzrecv.at[z, :, side],
-                      wz_s.at[off, i], wz_r.at[off, i], at_z(zt)))
-        wzrecv[z, :, side] = wz[own_slice, side]
-
-    weight_ring(0)
+
+    for i in range(2, PIECES):
+        weight_ring(i)
+
     for off in range(1, NZ):
         zs = mod(z - off, NZ)
         arrived(gall.at[c, pl.ds(pl.multiple_of(zs * 32, 32), 32)], rb_r.at[off])
     go(remote(gall.at[c], gall.at[c], core_s.at[5], core_r.at[5], partner))
-    weight_ring(1)
-
     for off in range(1, NZ):
         arrived(tgz.at[mod(z - off, NZ)], tz_r.at[off])
     ring_table = tgz[0]
@@ -511,7 +509,7 @@
     square = jnp.concatenate([table, jnp.zeros((size - CODES, size), F32)], axis=0)
     tg_ref[...] = square.T[:heads, :CODES] * (1.0 / math.sqrt(tokens * levels))
 
-    for i in range(2):
+    for i in range(PIECES):
         for off in range(1, NZ):
             arrived(wzrecv.at[mod(z - off, NZ), :, sides[i]], wz_r.at[off, i])
         weight = wzrecv[0, :, sides[i]].astype(F32)
@@ -552,7 +550,7 @@
 
     scratch = [
         bf(rows, 512), bf(rows, 512), bf(rows, 512), bf(512, 2048), dma((5,)),
-        pltpu.SemaphoreType.REGULAR((4,)), f32(4, rows, 768), bf(4, rows, 512), f32(4, 6, rows, 128), f32(4, rows, rows), f32(4, rows, rows),
+        pltpu.SemaphoreType.REGULAR((2,)), f32(4, rows, 768), bf(4, rows, 512), f32(4, 6, rows, 128), f32(4, rows, rows), f32(4, rows, rows),
         bf(4, rows, rows), bf(4, rows, 768), bf(rows, 512), bf(rows, 512),
         f32(rows, 512), f32(rows, 512), f32(rows, 512), f32(rows, 512),
         bf(512, 128), bf(512, 128), bf(256, 128), bf(NZ, 32, 128), bf(32, 128), bf(NX, 32, 128),
@@ -566,8 +564,8 @@
         f32(CODES, 128), f32(NX, CODES, 128),
         dma((6,)), dma((6,)), dma((6,)), dma((6,)), dma((NZ,)), dma((NZ,)), dma((NX,)), dma((NX,)),
         dma((NZ, 5)), dma((NZ, 5)), dma((NZ, 5)), dma((NZ, 5)), dma((NX,)), dma((NX,)),
-        dma((NZ,)), dma((NZ,)), dma((4,)), dma((4,)), dma((4,)), dma((4,)), dma((8,)), dma((8,)),
-        dma((NZ, 2)), dma((NZ, 2)), dma((NZ,)), dma((NZ,)), dma((NX,)), dma((NX,)),
+        dma((NZ,)), dma((NZ,)), dma((4,)), dma((4,)), dma((4,)), dma((4,)), dma((4 * PIECES,)), dma((4 * PIECES,)),
+        dma((NZ, PIECES)), dma((NZ, PIECES)), dma((NZ,)), dma((NZ,)), dma((NX,)), dma((NX,)),
     ]
     shape = jax.ShapeDtypeStruct
     results = pl.pallas_call(

time: 55.3 us -> 52.9 us (0.957); the launches traced: 55.1 us -> 52.1 us
  Pallas kernels: 53.1 us -> 50 us
    pallas_call x1, Pallas kernels: 52 us -> 49 us  [per_device(): pl.pallas_call(kernel, out_shape=(shape((rows, width), BF16), shape((32,...]
where the time goes in v4:
time: 52.9 us; the launch traced here: 52.1 us
  Pallas kernels  50 us (95%)
  local copies, waits for them, and re-layouts  1.39 us (3%)
  between operations  0.65 us (1%)
    pallas_call x1, Pallas kernels, per_device(): pl.pallas_call(kernel, out_shape=(shape((rows, width), BF16), shape((32,...  49 us
    unnamed x4, local copies, waits for them, and re-layouts  1.39 us

profile of v4, /device:TPU:1, one launch (start us, length us, event | category | flops | bytes accessed | tf_op | source)
XLA Modules:
  0.0 52.1 jit_solution(9731314516105238329)
XLA Ops:
  0.6 0.0 copy-start
  0.6 0.7 %copy-done = s32[256,9]{0,1:T(8,128)S(1)} copy-done((s32[256,9]{0,1:T(8,128)S(1)}, s32[256,9]{0,1:T(8,128)}, u32[]{:S(2)}) %copy-start) | copy-done | bytes 9240
  1.4 0.0 copy-start.1
  1.4 0.7 %copy-done.1 = f32[16,4]{0,1:T(4,128)S(1)} copy-done((f32[16,4]{0,1:T(4,128)S(1)}, f32[16,4]{0,1:T(4,128)}, u32[]{:S(2)}) %copy-start.1) | copy-done | bytes 280
  2.0 49.0 %layer.1 = (bf16[256,512]{1,0:T(8,128)(2,1)S(1)}, f32[32,512]{1,0:T(8,128)S(1)}, bf16[256,512]{1,0:T(8,128)(2,1)S(1)}, bf16[256,512]{1,0:T(8,128)(2,1)S(1)}, bf1...) custom-call(bf16[256,512]{1,0:T(8,128)(2,1)} %q_hbm.1, bf16[256,512]{1,0:T(8,128)(2,1)} %k_hbm.1, bf16[256,512]{1,0:T(8,128)(2,1)} %v_hbm.1, ...), custom_call_target="tpu_custom_call" | custom-call | tf_op jit(solution)/shard_map/layer/pallas_call | solution.py:571
  51.0 1.0 %store.1 = (bf16[256,512]{1,0:T(8,128)(2,1)}, f32[32,512]{1,0:T(8,128)}, bf16[256,512]{1,0:T(8,128)(2,1)}, bf16[256,512]{1,0:T(8,128)(2,1)}, bf16[256,512]{1,0:T(8,128)(2,1)}, /*index=5*/f32[4,16]{1,0:T(4,128)}) custom-call(bf16[256,512]{1,0:T(8,128)(2,1)S(1)} %get-tuple-element.18.refs_0_, f32[32,512]{1,0:T(8,128)S(1)} %get-tuple-element.19.refs_1_, ...), custom_call_target="tpu_custom_call" | custom-call | tf_op jit(solution)/shard_map/store/pallas_call | solution.py:589
Async XLA Ops:
  0.6 0.7 %copy-start = (s32[256,9]{0,1:T(8,128)S(1)}, s32[256,9]{0,1:T(8,128)}, u32[]{:S(2)}) copy-start(s32[256,9]{0,1:T(8,128)} %param.11) | copy-start | bytes 27652
  1.4 0.7 %copy-start.1 = (f32[16,4]{0,1:T(4,128)S(1)}, f32[16,4]{0,1:T(4,128)}, u32[]{:S(2)}) copy-start(f32[16,4]{0,1:T(4,128)} %param.10) | copy-start | bytes 772

commit v5 on v4

--- a/solution.py
+++ b/solution.py
@@ -396,11 +396,25 @@
 
     local_back(3)
     weight_relay(1)
+    for h in range(heads):
+        grad = gbuf[:, col(h)].astype(F32)
+        total = table_parts[h]
+        for l in range(6):
+            total = total + scales[l + 3] * mm(one_hot[l + 3], (grad * reads[h, :, col(l)]).astype(BF16), NN)
+        table_parts[h] = total
+    lane128 = lax.broadcasted_iota(jnp.int32, (CODES, size), 1)
+    partial_table = jnp.zeros((CODES, size), F32)
+    for h in range(heads):
+        summed = jnp.sum(table_parts[h], axis=1, keepdims=True)
+        partial_table = jnp.where(lane128 == h, summed, partial_table)
+    tgsend[...] = partial_table
+    go(remote(tgsend, tgcore, core_s.at[4], core_r.at[4], partner))
+
+    for i in range(2, PIECES):
+        weight_relay(i)
+
     weight_part(3, x)
     product_for(y)
-    for i in range(2, PIECES):
-        weight_relay(i)
-
     for off in range(1, NX):
         xs = mod(x - off, NX)
         arrived(xrecv_b.at[xs], xb_r.at[off], xs > x)
@@ -425,6 +439,12 @@
         go(remote(gsend.at[zt], gall.at[c, own_slice], rb_s.at[off], rb_r.at[off], at_z(zt)))
     gall[c, own_slice, :] = gsend[z]
 
+    arrived(tgcore, core_r.at[4])
+    tgzsend[...] = tgsend[...] + tgcore[...]
+    for off in range(1, NZ):
+        go(remote(tgzsend, tgz.at[z], tz_s.at[off], tz_r.at[off], at_z(mod(z + off, NZ))))
+    tgz[z] = tgzsend[...]
+
     def weight_ring(i):
         side = sides[i]
         arrived(wxrecv.at[0, :, side], wx_r.at[4 * i + 2])
@@ -448,27 +468,9 @@
     go(remote(mpart.at[right], mrecv.at[1], m_s.at[3], m_r.at[3], at_y(right)))
 
     for h in range(heads):
-        grad = gbuf[:, col(h)].astype(F32)
-        total = table_parts[h]
-        for l in range(6):
-            total = total + scales[l + 3] * mm(one_hot[l + 3], (grad * reads[h, :, col(l)]).astype(BF16), NN)
-        table_parts[h] = total
         qg_ref[:, col(h)] = (qgl[:, col(h)] + mm(sgbuf[h], found_states(h), NT)).astype(BF16)
-    lane128 = lax.broadcasted_iota(jnp.int32, (CODES, size), 1)
-    partial_table = jnp.zeros((CODES, size), F32)
-    for h in range(heads):
-        summed = jnp.sum(table_parts[h], axis=1, keepdims=True)
-        partial_table = jnp.where(lane128 == h, summed, partial_table)
-    tgsend[...] = partial_table
-    go(remote(tgsend, tgcore, core_s.at[4], core_r.at[4], partner))
 
     weight_ring(1)
-    arrived(tgcore, core_r.at[4])
-    tgzsend[...] = tgsend[...] + tgcore[...]
-    for off in range(1, NZ):
-        go(remote(tgzsend, tgz.at[z], tz_s.at[off], tz_r.at[off], at_z(mod(z + off, NZ))))
-    tgz[z] = tgzsend[...]
-
     for i in range(2, PIECES):
         weight_ring(i)
 

time: 52.9 us -> 50.7 us (0.958)
  the two profiles are of different devices: /device:TPU:1 before, /device:TPU:4 now
where the time goes in v5:
time: 50.7 us; the launch traced here: 50.5 us
  Pallas kernels  48.4 us (95%)
  local copies, waits for them, and re-layouts  1.39 us (3%)
  between operations  0.65 us (1%)
    pallas_call x1, Pallas kernels, per_device(): pl.pallas_call(kernel, out_shape=(shape((rows, width), BF16), shape((32,...  47.4 us
    unnamed x4, local copies, waits for them, and re-layouts  1.39 us
    pallas_call x1, Pallas kernels, per_device(): pl.pallas_call(store, out_shape=tuple((shape(value.shape, value.dtype) fo...  1.04 us

profile of v5, /device:TPU:4, one launch (start us, length us, event | category | flops | bytes accessed | tf_op | source)
XLA Modules:
  0.0 50.5 jit_solution(2226776874692239742)
XLA Ops:
  0.6 0.0 copy-start
  0.6 0.7 %copy-done = s32[256,9]{0,1:T(8,128)S(1)} copy-done((s32[256,9]{0,1:T(8,128)S(1)}, s32[256,9]{0,1:T(8,128)}, u32[]{:S(2)}) %copy-start) | copy-done | bytes 9240
  1.4 0.0 copy-start.1
  1.4 0.7 %copy-done.1 = f32[16,4]{0,1:T(4,128)S(1)} copy-done((f32[16,4]{0,1:T(4,128)S(1)}, f32[16,4]{0,1:T(4,128)}, u32[]{:S(2)}) %copy-start.1) | copy-done | bytes 280
  2.0 47.4 %layer.1 = (bf16[256,512]{1,0:T(8,128)(2,1)S(1)}, f32[32,512]{1,0:T(8,128)S(1)}, bf16[256,512]{1,0:T(8,128)(2,1)S(1)}, bf16[256,512]{1,0:T(8,128)(2,1)S(1)}, bf1...) custom-call(bf16[256,512]{1,0:T(8,128)(2,1)} %q_hbm.1, bf16[256,512]{1,0:T(8,128)(2,1)} %k_hbm.1, bf16[256,512]{1,0:T(8,128)(2,1)} %v_hbm.1, ...), custom_call_target="tpu_custom_call" | custom-call | tf_op jit(solution)/shard_map/layer/pallas_call | solution.py:573
  49.4 1.0 %store.1 = (bf16[256,512]{1,0:T(8,128)(2,1)}, f32[32,512]{1,0:T(8,128)}, bf16[256,512]{1,0:T(8,128)(2,1)}, bf16[256,512]{1,0:T(8,128)(2,1)}, bf16[256,512]{1,0:T(8,128)(2,1)}, /*index=5*/f32[4,16]{1,0:T(4,128)}) custom-call(bf16[256,512]{1,0:T(8,128)(2,1)S(1)} %get-tuple-element.18.refs_0_, f32[32,512]{1,0:T(8,128)S(1)} %get-tuple-element.19.refs_1_, ...), custom_call_target="tpu_custom_call" | custom-call | tf_op jit(solution)/shard_map/store/pallas_call | solution.py:591
Async XLA Ops:
  0.6 0.7 %copy-start = (s32[256,9]{0,1:T(8,128)S(1)}, s32[256,9]{0,1:T(8,128)}, u32[]{:S(2)}) copy-start(s32[256,9]{0,1:T(8,128)} %param.11) | copy-start | bytes 27652
  1.4 0.7 %copy-start.1 = (f32[16,4]{0,1:T(4,128)S(1)}, f32[16,4]{0,1:T(4,128)}, u32[]{:S(2)}) copy-start(f32[16,4]{0,1:T(4,128)} %param.10) | copy-start | bytes 772

commit v6 on v5

--- a/solution.py
+++ b/solution.py
@@ -321,9 +321,6 @@
 
     sides = [pl.ds(128 * i, 128) for i in range(PIECES)]
     weight_part(0, x_opposite)
-    product_for(opposite)
-    go(remote(mpart.at[opposite, top], mrelay.at[0], m_s.at[0], m_r.at[0], at_y(left)))
-    go(remote(mpart.at[opposite, low], mrelay.at[1], m_s.at[1], m_r.at[1], at_y(right)))
     weight_part(1, x_left)
     weight_chip(0, x_opposite)
     for i in range(PIECES):
@@ -331,6 +328,9 @@
                   wx_s.at[4 * i], wx_r.at[4 * i], at_x(x_left)))
         go(remote(wpart.at[x_opposite, c, low, sides[i]], wrelay.at[1, :, sides[i]],
                   wx_s.at[4 * i + 1], wx_r.at[4 * i + 1], at_x(x_right)))
+    product_for(opposite)
+    go(remote(mpart.at[opposite, top], mrelay.at[0], m_s.at[0], m_r.at[0], at_y(left)))
+    go(remote(mpart.at[opposite, low], mrelay.at[1], m_s.at[1], m_r.at[1], at_y(right)))
     weight_part(2, x_right)
     product_for(left)
     product_for(right)
@@ -467,10 +467,9 @@
     mpart[right, low] = (mpart[right, low].astype(F32) + mrelay[1].astype(F32)).astype(BF16)
     go(remote(mpart.at[right], mrecv.at[1], m_s.at[3], m_r.at[3], at_y(right)))
 
+    weight_ring(1)
     for h in range(heads):
         qg_ref[:, col(h)] = (qgl[:, col(h)] + mm(sgbuf[h], found_states(h), NT)).astype(BF16)
-
-    weight_ring(1)
     for i in range(2, PIECES):
         weight_ring(i)
 

time: 50.7 us -> 50.8 us (level)
  no operation moved by 1% of the time
where the time goes in v6:
time: 50.8 us; the launch traced here: 50.6 us
  Pallas kernels  48.6 us (96%)
  local copies, waits for them, and re-layouts  1.39 us (3%)
  between operations  0.65 us (1%)
    pallas_call x1, Pallas kernels, per_device(): pl.pallas_call(kernel, out_shape=(shape((rows, width), BF16), shape((32,...  47.5 us
    unnamed x4, local copies, waits for them, and re-layouts  1.39 us
    pallas_call x1, Pallas kernels, per_device(): pl.pallas_call(store, out_shape=tuple((shape(value.shape, value.dtype) fo...  1.04 us

profile of v6, /device:TPU:4, one launch (start us, length us, event | category | flops | bytes accessed | tf_op | source)
XLA Modules:
  0.0 50.6 jit_solution(7409692110597218327)
XLA Ops:
  0.6 0.0 copy-start
  0.6 0.7 %copy-done = s32[256,9]{0,1:T(8,128)S(1)} copy-done((s32[256,9]{0,1:T(8,128)S(1)}, s32[256,9]{0,1:T(8,128)}, u32[]{:S(2)}) %copy-start) | copy-done | bytes 9240
  1.4 0.0 copy-start.1
  1.4 0.7 %copy-done.1 = f32[16,4]{0,1:T(4,128)S(1)} copy-done((f32[16,4]{0,1:T(4,128)S(1)}, f32[16,4]{0,1:T(4,128)}, u32[]{:S(2)}) %copy-start.1) | copy-done | bytes 280
  2.0 47.5 %layer.1 = (bf16[256,512]{1,0:T(8,128)(2,1)S(1)}, f32[32,512]{1,0:T(8,128)S(1)}, bf16[256,512]{1,0:T(8,128)(2,1)S(1)}, bf16[256,512]{1,0:T(8,128)(2,1)S(1)}, bf1...) custom-call(bf16[256,512]{1,0:T(8,128)(2,1)} %q_hbm.1, bf16[256,512]{1,0:T(8,128)(2,1)} %k_hbm.1, bf16[256,512]{1,0:T(8,128)(2,1)} %v_hbm.1, ...), custom_call_target="tpu_custom_call" | custom-call | tf_op jit(solution)/shard_map/layer/pallas_call | solution.py:572
  49.6 1.0 %store.1 = (bf16[256,512]{1,0:T(8,128)(2,1)}, f32[32,512]{1,0:T(8,128)}, bf16[256,512]{1,0:T(8,128)(2,1)}, bf16[256,512]{1,0:T(8,128)(2,1)}, bf16[256,512]{1,0:T(8,128)(2,1)}, /*index=5*/f32[4,16]{1,0:T(4,128)}) custom-call(bf16[256,512]{1,0:T(8,128)(2,1)S(1)} %get-tuple-element.18.refs_0_, f32[32,512]{1,0:T(8,128)S(1)} %get-tuple-element.19.refs_1_, ...), custom_call_target="tpu_custom_call" | custom-call | tf_op jit(solution)/shard_map/store/pallas_call | solution.py:590
Async XLA Ops:
  0.6 0.7 %copy-start = (s32[256,9]{0,1:T(8,128)S(1)}, s32[256,9]{0,1:T(8,128)}, u32[]{:S(2)}) copy-start(s32[256,9]{0,1:T(8,128)} %param.11) | copy-start | bytes 27652
  1.4 0.7 %copy-start.1 = (f32[16,4]{0,1:T(4,128)S(1)}, f32[16,4]{0,1:T(4,128)}, u32[]{:S(2)}) copy-start(f32[16,4]{0,1:T(4,128)} %param.10) | copy-start | bytes 772
